TPU v7x, 128 devices: a whole 4x4x4 slice. The times are simulated.
128 devices in a mesh: mem: 4 (over z_hi, core), tile: 32 (over z_lo, y, x).
Axes of the slice: x: 4, y: 4, z: 4 (z_hi: 2, z_lo: 2; z = z_hi * 2 + z_lo), core: 2. Of those that a mesh axis runs over, the one named last changes fastest.
Arguments:
- gradient: float32 [4, 1024, 1024], P(None, 'tile', 'mem'), may hold values from -6 to 6
- static_scale: float32 [4, 1024, 1024], P(None, 'tile', 'mem'), may hold values from 0.5 to 2
- static_rate: float32 [4], replicated, may hold values from 0.05 to 0.24
- interp_index: int32 [4, 512, 512], P(None, 'tile', 'mem'), may hold values from 0 to 15
- interp_weight: float32 [4, 512, 512], P(None, 'tile', 'mem'), may hold values from 0.1 to 0.4
- members: bfloat16 [80, 4, 512, 512], P('mem', None, 'tile'), may hold values from -6 to 6
- spread_rate: float32 [512, 512], P('tile'), may hold values from 0.02 to 0.24
Outputs:
- hybrid: float32 [4, 1024, 1024], P(None, 'tile', 'mem')
Inputs may be any that keep to these rules, and one draw needn't show every extreme that they name: `interp_index`: the fine cell (a, b) of a coarse cell's 4 x 4 block, numbered 4 * a + b; slots may name the same cell.
All inputs are finite; a program needn't handle non-finite values.
Results may differ from a plain program's by a relative error of at most 0.0003.
Values sent between devices are 32-bit elements; how exact they have to be, the bound alone decides.
A program may use at most 128 MiB of HBM per device.

v0:
```python
import jax
import jax.numpy as jnp
from jax import lax
from jax.sharding import PartitionSpec as P

STATIC_PASSES = 4
SPREAD_PASSES = 8


def padded_2(array, sides, width):
    edges = {}
    for axis, dim in sides:
        size, length = (lax.axis_size(axis), array.shape[dim])
        up = [(i, (i + 1) % size) for i in range(size - 1)]
        last = lax.slice_in_dim(array, length - width, length, axis=dim)
        first = lax.slice_in_dim(array, 0, width, axis=dim)
        edges[dim] = (
            lax.ppermute(last, axis, up),
            lax.ppermute(first, axis, [(b, a) for a, b in up]),
        )
    done = []
    for _, dim in sides:
        low, high = edges[dim]
        around = [(width, width) if d in done else (0, 0) for d in range(array.ndim)]
        array = jnp.concatenate([jnp.pad(low, around), array, jnp.pad(high, around)], axis=dim)
        done.append(dim)
    return array


def with_halo(block, sides, width):
    for axis, dim in sides:
        count = lax.axis_size(axis)
        forward = [(i, i + 1) for i in range(count - 1)]
        backward = [(target, source) for source, target in forward]
        low = lax.ppermute(
            lax.slice_in_dim(block, block.shape[dim] - width, None, axis=dim), axis, forward
        )
        high = lax.ppermute(lax.slice_in_dim(block, 0, width, axis=dim), axis, backward)
        block = jnp.concatenate([low, block, high], axis=dim)
    return block


def laid_out(tiles, dim):
    tiles = jnp.moveaxis(tiles, 0, dim)
    dims = tiles.shape
    return tiles.reshape(*dims[:dim], dims[dim] * dims[dim + 1], *dims[dim + 2 :])


def copy_for_each(array, axis):
    copies = jnp.broadcast_to(array, (lax.axis_size(axis), *array.shape))
    return lax.all_to_all(copies, axis, split_axis=0, concat_axis=0, tiled=True)


def gather_directly(array, axis, dim):
    return laid_out(copy_for_each(array, axis), dim)


def cut_along(array, dim, length):
    before, after = (array.shape[:dim], array.shape[dim + 1 :])
    return jnp.moveaxis(array.reshape(*before, length, -1, *after), dim, 0)


def sent_and_summed(array, axis, dim):
    length = lax.axis_size(axis)
    tiles = lax.all_to_all(cut_along(array, dim, length), axis, 0, 0, tiled=True)
    return jnp.sum(tiles, axis=0)


def pad_edges(values, margin):
    return jnp.pad(values, [(0, 0)] * (values.ndim - 2) + [(margin, margin), (margin, margin)])


def diffuse(padded, rate_field):
    centre = padded[..., 1:-1, 1:-1]
    beside = (
        padded[..., 2:, 1:-1]
        + padded[..., :-2, 1:-1]
        + padded[..., 1:-1, 2:]
        + padded[..., 1:-1, :-2]
    )
    return centre + rate_field * (beside - 4.0 * centre)


def weights_table(slot_index, slot_weight):
    offsets = jnp.arange(16, dtype=jnp.int32)[:, None, None]
    offset_table = jnp.zeros((16,) + slot_index.shape[1:], jnp.float32)
    for slot_number in range(slot_index.shape[0]):
        offset_table = offset_table + jnp.where(
            slot_index[slot_number][None] == offsets, slot_weight[slot_number][None], 0.0
        )
    return offset_table


def restrict(padded, offset_table):
    fields = padded.shape[0]
    height = (padded.shape[1] - 4) // 2
    breadth = (padded.shape[2] - 4) // 2
    parity = padded.reshape(fields, height + 2, 2, breadth + 2, 2)
    accumulated = jnp.zeros((fields, height, breadth), jnp.float32)
    for row_shift in range(4):
        row_block = (row_shift + 1) // 2
        row_parity = (row_shift + 1) % 2
        for col_shift in range(4):
            col_block = (col_shift + 1) // 2
            col_parity = (col_shift + 1) % 2
            picked = parity[
                :,
                row_block : row_block + height,
                row_parity,
                col_block : col_block + breadth,
                col_parity,
            ]
            accumulated = accumulated + offset_table[4 * row_shift + col_shift] * picked
    return accumulated


def prolong(contrib):
    fields = contrib.shape[1]
    height = contrib.shape[2]
    breadth = contrib.shape[3]
    rows_out = []
    for row_parity in range(2):
        cols_out = []
        for col_parity in range(2):
            total = jnp.zeros((fields, height + 1, breadth + 1), jnp.float32)
            for row_block in range(2):
                for col_block in range(2):
                    piece = contrib[4 * (2 * row_block + row_parity) + 2 * col_block + col_parity]
                    total = total + jnp.pad(
                        piece, ((0, 0), (row_block, 1 - row_block), (col_block, 1 - col_block))
                    )
            cols_out.append(total)
        rows_out.append(jnp.stack(cols_out, axis=-1))
    placed = jnp.stack(rows_out, axis=2)
    return placed.reshape(fields, 2 * height + 2, 2 * breadth + 2)


def local(gradient, static_scale, static_rate, interp_index, interp_weight, members, spread_rate):
    smooth = static_scale * gradient
    for repeat in range(STATIC_PASSES):
        padded = padded_2(smooth, (("mem", 2), ("tile", 1)), 1)
        smooth = diffuse(padded, static_rate[:, None, None])
    static = static_scale * smooth
    offset_table = weights_table(interp_index, interp_weight)
    rimmed = with_halo(gradient, (("mem", 2), ("tile", 1)), 2)
    local_coarse = restrict(rimmed, offset_table)
    coarse = gather_directly(local_coarse, "mem", 2)
    member_count, fields, height, breadth = members.shape
    perturbed = members.astype(jnp.float32)
    values = (perturbed * coarse[None]).reshape(member_count * fields, height, breadth)
    stacked = jnp.concatenate([values, spread_rate[None]], axis=0)
    widened = with_halo(stacked, (("tile", 1),), SPREAD_PASSES)
    wide_rate = widened[-1]
    wide_values = widened[:-1]
    for repeat in range(SPREAD_PASSES):
        wide_values = diffuse(pad_edges(wide_values, 1), wide_rate)
    values = wide_values[:, SPREAD_PASSES : SPREAD_PASSES + height]
    values = values.reshape(member_count, fields, height, breadth)
    partial_value = jnp.sum(perturbed * values, axis=0)
    members_all = member_count * lax.axis_size("mem")
    my_share = sent_and_summed(partial_value, "mem", 2)
    ensemble = my_share / (members_all - 1)
    contrib = offset_table[:, None] * ensemble[None]
    contrib = with_halo(contrib, (("mem", 3), ("tile", 2)), 1)
    spread = prolong(contrib)
    fine_height = gradient.shape[1]
    fine_breadth = gradient.shape[2]
    fine_grid = spread[:, 3 : 3 + fine_height, 3 : 3 + fine_breadth]
    return 0.3 * static + 2.8 * fine_grid


def solution(mesh):
    return jax.shard_map(
        local,
        mesh=mesh,
        in_specs=(
            P(None, "tile", "mem"),
            P(None, "tile", "mem"),
            P(),
            P(None, "tile", "mem"),
            P(None, "tile", "mem"),
            P("mem", None, "tile", None),
            P("tile", None),
        ),
        out_specs=P(None, "tile", "mem"),
        check_vma=False,
    )
```

profile of v0, /device:TPU:33, one launch (start us, length us, event | category | flops | bytes accessed | tf_op | source)
XLA Modules:
  0.0 271.6 jit_solution(1327435482212314487)
XLA Ops:
  1.0 5.2 %collective-permute-start.16 = (f32[4,32,2]{2,1,0:T(8,128)S(1)}, f32[4,32,2]{2,1,0:T(8,128)S(1)}, u32[]{:S(2)}, u32[]{:S(2)}) collective-permute-start(f32[4,32,2]{2,1,0:T(8,128)S(1)} %get-tuple-element.81), channel_id=1, source_target_pairs={{0,32},{32,64},{64,96},{1,33},{33,65},{65,97},{2,34},{34,66},{66,9... | collective-permute-start | bytes 3080 | tf_op jit(solution)/shard_map/ppermute | solution.py:35
  6.1 1.9 collective-permute-start.17
  9.1 5.1 %collective-permute-start = (f32[4,32,1]{2,1,0:T(8,128)S(1)}, f32[4,32,1]{2,1,0:T(8,128)S(1)}, u32[]{:S(2)}, u32[]{:S(2)}) collective-permute-start(f32[4,32,1]{2,1,0:T(8,128)S(1)} %get-tuple-element.64), channel_id=1, source_target_pairs={{0,32},{32,64},{64,96},{1,33},{33,65},{65,97},{2,34},{34,66},{66,9... | collective-permute-start | bytes 1544 | tf_op jit(solution)/shard_map/ppermute | solution.py:18
  14.3 1.9 collective-permute-start.1
  18.7 3.1 %collective-permute-start.18 = (f32[4,2,260]{2,1,0:T(2,128)S(1)}, f32[4,2,260]{2,1,0:T(2,128)S(1)}, u32[]{:S(2)}, u32[]{:S(2)}) collective-permute-start(f32[4,2,260]{2,1,0:T(2,128)S(1)} %get-tuple-element.47), channel_id=1, source_target_pairs={{0,1},{1,2},{2,3},{3,4},{4,5},{5,6},{6,7},{7,8},{8,9},{9,10},{10,1... | collective-permute-start | bytes 24968 | tf_op jit(solution)/shard_map/ppermute | solution.py:35
  21.8 6.4 %collective-permute-start.19 = (f32[4,2,260]{2,1,0:T(2,128)S(1)}, f32[4,2,260]{2,1,0:T(2,128)S(1)}, u32[]{:S(2)}, u32[]{:S(2)}) collective-permute-start(f32[4,2,260]{2,1,0:T(2,128)S(1)} %get-tuple-element.48), channel_id=1, source_target_pairs={{1,0},{2,1},{3,2},{4,3},{5,4},{6,5},{7,6},{8,7},{9,8},{10,9},{11,1... | collective-permute-start | bytes 24968 | tf_op jit(solution)/shard_map/ppermute | solution.py:38
  30.0 3.7 %copy.457 = f32[4,36,260]{0,2,1:T(8,128)} copy(f32[4,36,260]{2,1,0:T(8,128)S(1)} %pad_maximum_fusion.4) | data formatting | bytes 299520 | tf_op jit(solution)/shard_map/concatenate | solution.py:39
  33.7 6.8 %reshape.39 = f32[4,18,2,130,2]{0,4,3,2,1:T(2,128)} reshape(f32[4,36,260]{0,2,1:T(8,128)} %copy.457) | data formatting | bytes 299520 | tf_op jit(solution)/shard_map/reshape | solution.py:98
  40.5 23.9 %fusion.82 = (f32[4,16,1,128,1]{0,4,3,2,1:T(1,128)S(1)}, f32[4,16,1,128,1]{0,4,3,2,1:T(1,128)S(1)}, f32[4,16,1,128,1]{0,4,3,2,1:T(1,128)S(1)}, f32[4,16,1,128,1]...) fusion(f32[4,18,2,130,2]{0,4,3,2,1:T(2,128)} %reshape.39), kind=kLoop, calls=%fused_computation.223 | loop fusion | bytes 1048576 | tf_op jit(solution)/shard_map/slice | solution.py:106
  64.5 5.2 %multiply_add_fusion = f32[4,16,128]{0,2,1:T(8,128)S(1)} fusion(f32[4,16,128]{0,2,1:T(8,128)S(1)} %bitcast.168, f32[4,16,128]{0,2,1:T(8,128)S(1)} %bitcast.167, f32[4,16,128]{0,2,1:T(8,128)S(1)} %bitcast.169, f32[4,16,128]{0,2,1:T(8,128)S(1)} %bitcast.155, f32[4,16,128]{0,2,1:T(8,128)S(1)} %bitcast.156, f32[4,16,128]{0,2,1:T(8,128)S(1)} %bitcast.157, ...), kind=kLoop, calls=%fused_computation.89 | loop fusion | flops 253952 | bytes 688128 | tf_op jit(solution)/shard_map/add | solution.py:113
  70.6 6.0 %all-to-all-start = ((f32[4,4,16,128]{3,2,1,0:T(8,128)}), f32[4,4,16,128]{3,2,1,0:T(8,128)S(1)}, u32[]{:S(2)}, u32[]{:S(2)}) async-start(f32[4,4,16,128]{3,2,1,0:T(8,128)} %broadcast_in_dim.60), calls=%async_computation | async-start | bytes 262144 | tf_op jit(solution)/shard_map/all_to_all | solution.py:51
  76.7 8.7 %collective-permute-start.2 = (f32[4,1,256]{2,1,0:T(1,128)S(1)}, f32[4,1,256]{2,1,0:T(1,128)S(1)}, u32[]{:S(2)}, u32[]{:S(2)}) collective-permute-start(f32[4,1,256]{2,1,0:T(1,128)S(1)} %get-tuple-element.61), channel_id=1, source_target_pairs={{1,0},{2,1},{3,2},{4,3},{5,4},{6,5},{7,6},{8,7},{9,8},{10,9},{11,1... | collective-permute-start | bytes 12296 | tf_op jit(solution)/shard_map/ppermute | solution.py:19
  85.4 1.9 collective-permute-start.3
  88.1 1.9 collective-permute-start.20
  90.0 7.6 %collective-permute-start.21 = (f32[81,8,512]{2,1,0:T(8,128)S(1)}, f32[81,8,512]{2,1,0:T(8,128)S(1)}, u32[]{:S(2)}, u32[]{:S(2)}) collective-permute-start(f32[81,8,512]{2,1,0:T(8,128)S(1)} %get-tuple-element.26), channel_id=1, source_target_pairs={{1,0},{2,1},{3,2},{4,3},{5,4},{6,5},{7,6},{8,7},{9,8},{10,9},{11,1... | collective-permute-start | bytes 3981320 | tf_op jit(solution)/shard_map/ppermute | solution.py:38
  97.9 3.4 %collective-permute-start.6 = (f32[4,1,256]{2,1,0:T(1,128)S(1)}, f32[4,1,256]{2,1,0:T(1,128)S(1)}, u32[]{:S(2)}, u32[]{:S(2)}) collective-permute-start(f32[4,1,256]{2,1,0:T(1,128)S(1)} %get-tuple-element.57), channel_id=1, source_target_pairs={{1,0},{2,1},{3,2},{4,3},{5,4},{6,5},{7,6},{8,7},{9,8},{10,9},{11,1... | collective-permute-start | bytes 12296 | tf_op jit(solution)/shard_map/ppermute | solution.py:19
  101.2 1.9 collective-permute-start.7
  103.3 5.8 %collective-permute-start.4 = (f32[4,32,1]{2,1,0:T(8,128)S(1)}, f32[4,32,1]{2,1,0:T(8,128)S(1)}, u32[]{:S(2)}, u32[]{:S(2)}) collective-permute-start(f32[4,32,1]{2,1,0:T(8,128)S(1)} %get-tuple-element.60), channel_id=1, source_target_pairs={{0,32},{32,64},{64,96},{1,33},{33,65},{65,97},{2,34},{34,66},{66,9... | collective-permute-start | bytes 1544 | tf_op jit(solution)/shard_map/ppermute | solution.py:18
  110.4 1.9 collective-permute-start.5
  112.3 6.1 %collective-permute-done.5 = f32[4,32,1]{2,1,0:T(8,128)S(1)} collective-permute-done((f32[4,32,1]{2,1,0:T(8,128)S(1)}, f32[4,32,1]{2,1,0:T(8,128)S(1)}, u32[]{:S(2)}, u32[]{:S(2)}) %collective-permute-start.5) | collective-permute-done | bytes 544 | tf_op jit(solution)/shard_map/ppermute | solution.py:19
  118.4 7.2 %collective-permute-done.6 = f32[4,1,256]{2,1,0:T(1,128)S(1)} collective-permute-done((f32[4,1,256]{2,1,0:T(1,128)S(1)}, f32[4,1,256]{2,1,0:T(1,128)S(1)}, u32[]{:S(2)}, u32[]{:S(2)}) %collective-permute-start.6) | collective-permute-done | bytes 4128 | tf_op jit(solution)/shard_map/ppermute | solution.py:19
  125.9 5.5 %collective-permute-start.8 = (f32[4,32,1]{2,1,0:T(8,128)S(1)}, f32[4,32,1]{2,1,0:T(8,128)S(1)}, u32[]{:S(2)}, u32[]{:S(2)}) collective-permute-start(f32[4,32,1]{2,1,0:T(8,128)S(1)} %get-tuple-element.56), channel_id=1, source_target_pairs={{0,32},{32,64},{64,96},{1,33},{33,65},{65,97},{2,34},{34,66},{66,9... | collective-permute-start | bytes 1544 | tf_op jit(solution)/shard_map/ppermute | solution.py:18
  131.4 1.9 collective-permute-start.9
  133.3 9.0 %collective-permute-start.10 = (f32[4,1,256]{2,1,0:T(1,128)S(1)}, f32[4,1,256]{2,1,0:T(1,128)S(1)}, u32[]{:S(2)}, u32[]{:S(2)}) collective-permute-start(f32[4,1,256]{2,1,0:T(1,128)S(1)} %get-tuple-element.53), channel_id=1, source_target_pairs={{1,0},{2,1},{3,2},{4,3},{5,4},{6,5},{7,6},{8,7},{9,8},{10,9},{11,1... | collective-permute-start | bytes 12296 | tf_op jit(solution)/shard_map/ppermute | solution.py:19
  142.4 1.9 collective-permute-start.11
  145.6 4.7 %fusion.5 = f32[80,32,512]{2,1,0:T(8,128)S(1)} fusion(f32[80,32,512]{2,1,0:T(8,128)S(1)} %slice.610, f32[32,512]{1,0:T(8,128)S(1)} %maximum_bitcast_fusion.2), kind=kLoop, calls=%fused_computation.38 | loop fusion | flops 9175040 | bytes 10551296 | tf_op jit(solution)/shard_map/add | solution.py:81
  150.3 4.5 %fusion.11 = f32[80,32,512]{2,1,0:T(8,128)S(1)} fusion(f32[80,32,512]{2,1,0:T(8,128)S(1)} %fusion.5, f32[32,512]{1,0:T(8,128)S(1)} %maximum_bitcast_fusion.2), kind=kLoop, calls=%fused_computation.44 | loop fusion | flops 9175040 | bytes 10551296 | tf_op jit(solution)/shard_map/add | solution.py:81
  154.8 4.5 %fusion.17 = f32[80,32,512]{2,1,0:T(8,128)S(1)} fusion(f32[80,32,512]{2,1,0:T(8,128)S(1)} %fusion.11, f32[32,512]{1,0:T(8,128)S(1)} %maximum_bitcast_fusion.2), kind=kLoop, calls=%fused_computation.50 | loop fusion | flops 9175040 | bytes 10551296 | tf_op jit(solution)/shard_map/add | solution.py:81
  159.3 4.5 %fusion.23 = f32[80,32,512]{2,1,0:T(8,128)S(1)} fusion(f32[80,32,512]{2,1,0:T(8,128)S(1)} %fusion.17, f32[32,512]{1,0:T(8,128)S(1)} %maximum_bitcast_fusion.2), kind=kLoop, calls=%fused_computation.56 | loop fusion | flops 9175040 | bytes 10551296 | tf_op jit(solution)/shard_map/add | solution.py:81
  163.8 6.1 %fusion.29 = f32[80,32,512]{2,1,0:T(8,128)} fusion(f32[80,32,512]{2,1,0:T(8,128)S(1)} %fusion.23, f32[32,512]{1,0:T(8,128)S(1)} %maximum_bitcast_fusion.2), kind=kLoop, calls=%fused_computation.62 | loop fusion | flops 9175040 | bytes 10551296 | tf_op jit(solution)/shard_map/add | solution.py:81
  169.9 11.7 %fusion.35 = f32[80,32,512]{2,1,0:T(8,128)S(1)} fusion(f32[80,32,512]{2,1,0:T(8,128)} %fusion.29, f32[32,512]{1,0:T(8,128)S(1)} %maximum_bitcast_fusion.2), kind=kLoop, calls=%fused_computation.68 | loop fusion | flops 9175040 | bytes 10551296 | tf_op jit(solution)/shard_map/add | solution.py:81
  181.5 6.3 %fusion.41 = f32[80,32,512]{2,1,0:T(8,128)} fusion(f32[80,32,512]{2,1,0:T(8,128)S(1)} %fusion.35, f32[32,512]{1,0:T(8,128)S(1)} %maximum_bitcast_fusion.2), kind=kLoop, calls=%fused_computation.74 | loop fusion | flops 9175040 | bytes 10551296 | tf_op jit(solution)/shard_map/add | solution.py:81
  187.8 16.2 %pad_slice_fusion.3 = (f32[80,32,512]{2,1,0:T(8,128)}, f32[80,32,512]{2,1,0:T(8,128)}, f32[80,32,512]{2,1,0:T(8,128)}, f32[80,32,512]{2,1,0:T(8,128)}) fusion(f32[80,32,512]{2,1,0:T(8,128)} %fusion.41), kind=kLoop, calls=%fused_computation.3 | loop fusion | bytes 26214400 | tf_op jit(solution)/shard_map/slice | solution.py:76
  204.0 6.5 %fusion.45 = f32[80,16,512]{2,1,0:T(8,128)S(1)} fusion(f32[80,32,512]{2,1,0:T(8,128)} %get-tuple-element.8, f32[80,32,512]{2,1,0:T(8,128)} %get-tuple-element.7, f32[80,32,512]{2,1,0:T(8,128)} %get-tuple-element.6, f32[80,32,512]{2,1,0:T(8,128)} %get-tuple-element.5, f32[80,32,512]{2,1,0:T(8,128)} %fusion.41, f32[16,512]{1,0:T(8,128)S(1)} %slice-done), kind=kLoop, calls=%fused_computation.83 | loop fusion | flops 4587520 | bytes 15761408 | tf_op jit(solution)/shard_map/add | solution.py:81
  211.7 4.6 %all-to-all-start.1 = ((f32[4,4,16,128]{3,2,1,0:T(8,128)}), f32[4,4,16,128]{3,2,1,0:T(8,128)S(1)}, u32[]{:S(2)}, u32[]{:S(2)}) async-start(f32[4,4,16,128]{3,2,1,0:T(8,128)} %copy.476), calls=%async_computation.1 | async-start | bytes 262144 | tf_op jit(solution)/shard_map/all_to_all | solution.py:65
  216.5 4.8 %all-to-all-done.1 = f32[4,4,16,128]{3,2,1,0:T(8,128)S(1)} async-done(((f32[4,4,16,128]{3,2,1,0:T(8,128)}), f32[4,4,16,128]{3,2,1,0:T(8,128)S(1)}, u32[]{:S(2)}, u32[]{:S(2)}) %all-to-all-start.1) | async-done | bytes 131104 | tf_op jit(solution)/shard_map/all_to_all | solution.py:65
  221.9 2.9 %collective-permute-start.22 = (f32[16,4,16,1]{3,1,2,0:T(4,128)S(1)}, f32[16,4,16,1]{3,1,2,0:T(4,128)S(1)}, u32[]{:S(2)}, u32[]{:S(2)}) collective-permute-start(f32[16,4,16,1]{3,1,2,0:T(4,128)S(1)} %get-tuple-element.45), channel_id=1, source_target_pairs={{0,32},{32,64},{64,96},{1,33},{33,65},{65,97},{2,34},{34,66},{66,9... | collective-permute-start | bytes 12296 | tf_op jit(solution)/shard_map/ppermute | solution.py:35
  224.8 1.9 collective-permute-start.23
  226.9 4.1 %collective-permute-done.22 = f32[16,4,16,1]{3,1,2,0:T(4,128)S(1)} collective-permute-done((f32[16,4,16,1]{3,1,2,0:T(4,128)S(1)}, f32[16,4,16,1]{3,1,2,0:T(4,128)S(1)}, u32[]{:S(2)}, u32[]{:S(2)}) %collective-permute-start.22) | collective-permute-done | bytes 4128 | tf_op jit(solution)/shard_map/ppermute | solution.py:35
  230.9 5.9 %collective-permute-done.23 = f32[16,4,16,1]{3,1,2,0:T(4,128)S(1)} collective-permute-done((f32[16,4,16,1]{3,1,2,0:T(4,128)S(1)}, f32[16,4,16,1]{3,1,2,0:T(4,128)S(1)}, u32[]{:S(2)}, u32[]{:S(2)}) %collective-permute-start.23) | collective-permute-done | bytes 4128 | tf_op jit(solution)/shard_map/ppermute | solution.py:38
  237.0 1.9 collective-permute-start.24
  238.9 8.5 %collective-permute-start.25 = (f32[16,4,1,130]{3,1,2,0:T(4,128)S(1)}, f32[16,4,1,130]{3,1,2,0:T(4,128)S(1)}, u32[]{:S(2)}, u32[]{:S(2)}) collective-permute-start(f32[16,4,1,130]{3,1,2,0:T(4,128)S(1)} %get-tuple-element.28), channel_id=1, source_target_pairs={{1,0},{2,1},{3,2},{4,3},{5,4},{6,5},{7,6},{8,7},{9,8},{10,9},{11,1... | collective-permute-start | bytes 99848 | tf_op jit(solution)/shard_map/ppermute | solution.py:38
  247.4 1.9 collective-permute-start.12
  249.4 2.4 collective-permute-start.13
  251.8 3.4 %collective-permute-start.14 = (f32[4,1,256]{2,1,0:T(1,128)S(1)}, f32[4,1,256]{2,1,0:T(1,128)S(1)}, u32[]{:S(2)}, u32[]{:S(2)}) collective-permute-start(f32[4,1,256]{2,1,0:T(1,128)S(1)} %get-tuple-element.49), channel_id=1, source_target_pairs={{1,0},{2,1},{3,2},{4,3},{5,4},{6,5},{7,6},{8,7},{9,8},{10,9},{11,1... | collective-permute-start | bytes 12296 | tf_op jit(solution)/shard_map/ppermute | solution.py:19
  255.2 1.9 collective-permute-start.15
  258.8 5.8 %copy.481 = f32[4,19,2,131,2]{4,3,2,1,0:T(8,128)} copy(f32[4,19,2,131,2]{3,0,1,4,2:T(4,128)S(1)} %pad_maximum_fusion.3) | data formatting | bytes 318592 | tf_op jit(solution)/shard_map/reshape | solution.py:135
  264.7 6.0 %reshape.44 = f32[4,38,262]{2,1,0:T(8,128)S(1)} reshape(f32[4,19,2,131,2]{4,3,2,1,0:T(8,128)} %copy.481) | data formatting | bytes 318592 | tf_op jit(solution)/shard_map/reshape | solution.py:135
  (79 shorter events, 15.9 us)
Async XLA Ops:
  1.0 16.8 %collective-permute-start.16 = (f32[4,32,2]{2,1,0:T(8,128)S(1)}, f32[4,32,2]{2,1,0:T(8,128)S(1)}, u32[]{:S(2)}, u32[]{:S(2)}) collective-permute-start(f32[4,32,2]{2,1,0:T(8,128)S(1)} %get-tuple-element.81), channel_id=1, source_target_pairs={{0,32},{32,64},{64,96},{1,33},{33,65},{65,97},{2,34},{34,66},{66,9... | collective-permute-start | bytes 3080 | tf_op jit(solution)/shard_map/ppermute | solution.py:35
  6.1 11.6 %collective-permute-start.17 = (f32[4,32,2]{2,1,0:T(8,128)S(1)}, f32[4,32,2]{2,1,0:T(8,128)S(1)}, u32[]{:S(2)}, u32[]{:S(2)}) collective-permute-start(f32[4,32,2]{2,1,0:T(8,128)S(1)} %get-tuple-element.82), channel_id=1, source_target_pairs={{32,0},{64,32},{96,64},{33,1},{65,33},{97,65},{34,2},{66,34},{98,6... | collective-permute-start | bytes 3080 | tf_op jit(solution)/shard_map/ppermute | solution.py:38
  9.1 80.9 %collective-permute-start = (f32[4,32,1]{2,1,0:T(8,128)S(1)}, f32[4,32,1]{2,1,0:T(8,128)S(1)}, u32[]{:S(2)}, u32[]{:S(2)}) collective-permute-start(f32[4,32,1]{2,1,0:T(8,128)S(1)} %get-tuple-element.64), channel_id=1, source_target_pairs={{0,32},{32,64},{64,96},{1,33},{33,65},{65,97},{2,34},{34,66},{66,9... | collective-permute-start | bytes 1544 | tf_op jit(solution)/shard_map/ppermute | solution.py:18
  14.3 83.3 %collective-permute-start.1 = (f32[4,32,1]{2,1,0:T(8,128)S(1)}, f32[4,32,1]{2,1,0:T(8,128)S(1)}, u32[]{:S(2)}, u32[]{:S(2)}) collective-permute-start(f32[4,32,1]{2,1,0:T(8,128)S(1)} %get-tuple-element.63), channel_id=1, source_target_pairs={{32,0},{64,32},{96,64},{33,1},{65,33},{97,65},{34,2},{66,34},{98,6... | collective-permute-start | bytes 1544 | tf_op jit(solution)/shard_map/ppermute | solution.py:19
  18.7 9.5 %collective-permute-start.18 = (f32[4,2,260]{2,1,0:T(2,128)S(1)}, f32[4,2,260]{2,1,0:T(2,128)S(1)}, u32[]{:S(2)}, u32[]{:S(2)}) collective-permute-start(f32[4,2,260]{2,1,0:T(2,128)S(1)} %get-tuple-element.47), channel_id=1, source_target_pairs={{0,1},{1,2},{2,3},{3,4},{4,5},{5,6},{6,7},{7,8},{8,9},{9,10},{10,1... | collective-permute-start | bytes 24968 | tf_op jit(solution)/shard_map/ppermute | solution.py:35
  21.8 7.2 %collective-permute-start.19 = (f32[4,2,260]{2,1,0:T(2,128)S(1)}, f32[4,2,260]{2,1,0:T(2,128)S(1)}, u32[]{:S(2)}, u32[]{:S(2)}) collective-permute-start(f32[4,2,260]{2,1,0:T(2,128)S(1)} %get-tuple-element.48), channel_id=1, source_target_pairs={{1,0},{2,1},{3,2},{4,3},{5,4},{6,5},{7,6},{8,7},{9,8},{10,9},{11,1... | collective-permute-start | bytes 24968 | tf_op jit(solution)/shard_map/ppermute | solution.py:38
  64.4 22.9 %copy-start = (bf16[20,4,16,512]{3,2,1,0:T(8,128)(2,1)S(1)}, bf16[20,4,16,512]{3,2,1,0:T(8,128)(2,1)}, u32[]{:S(2)}) copy-start(bf16[20,4,16,512]{3,2,1,0:T(8,128)(2,1)} %param.12) | copy-start | bytes 3932164
  69.6 18.2 %copy-start.3 = (f32[16,512]{1,0:T(8,128)S(1)}, f32[16,512]{1,0:T(8,128)}, u32[]{:S(2)}) copy-start(f32[16,512]{1,0:T(8,128)} %param.13) | copy-start | bytes 98308
  70.0 27.7 %copy-start.4 = (f32[4]{0:T(128)S(1)}, f32[4]{0:T(128)}, u32[]{:S(2)}) copy-start(f32[4]{0:T(128)} %param.9) | copy-start | bytes 52
  70.6 16.7 %all-to-all-start = ((f32[4,4,16,128]{3,2,1,0:T(8,128)}), f32[4,4,16,128]{3,2,1,0:T(8,128)S(1)}, u32[]{:S(2)}, u32[]{:S(2)}) async-start(f32[4,4,16,128]{3,2,1,0:T(8,128)} %broadcast_in_dim.60), calls=%async_computation | async-start | bytes 262144 | tf_op jit(solution)/shard_map/all_to_all | solution.py:51
  76.7 20.9 %collective-permute-start.2 = (f32[4,1,256]{2,1,0:T(1,128)S(1)}, f32[4,1,256]{2,1,0:T(1,128)S(1)}, u32[]{:S(2)}, u32[]{:S(2)}) collective-permute-start(f32[4,1,256]{2,1,0:T(1,128)S(1)} %get-tuple-element.61), channel_id=1, source_target_pairs={{1,0},{2,1},{3,2},{4,3},{5,4},{6,5},{7,6},{8,7},{9,8},{10,9},{11,1... | collective-permute-start | bytes 12296 | tf_op jit(solution)/shard_map/ppermute | solution.py:19
  85.4 12.2 %collective-permute-start.3 = (f32[4,1,256]{2,1,0:T(1,128)S(1)}, f32[4,1,256]{2,1,0:T(1,128)S(1)}, u32[]{:S(2)}, u32[]{:S(2)}) collective-permute-start(f32[4,1,256]{2,1,0:T(1,128)S(1)} %get-tuple-element.62), channel_id=1, source_target_pairs={{0,1},{1,2},{2,3},{3,4},{4,5},{5,6},{6,7},{7,8},{8,9},{9,10},{10,1... | collective-permute-start | bytes 12296 | tf_op jit(solution)/shard_map/ppermute | solution.py:18
  88.1 54.3 %collective-permute-start.20 = (f32[81,8,512]{2,1,0:T(8,128)S(1)}, f32[81,8,512]{2,1,0:T(8,128)S(1)}, u32[]{:S(2)}, u32[]{:S(2)}) collective-permute-start(f32[81,8,512]{2,1,0:T(8,128)S(1)} %get-tuple-element.25), channel_id=1, source_target_pairs={{0,1},{1,2},{2,3},{3,4},{4,5},{5,6},{6,7},{7,8},{8,9},{9,10},{10,1... | collective-permute-start | bytes 3981320 | tf_op jit(solution)/shard_map/ppermute | solution.py:35
  90.0 54.3 %collective-permute-start.21 = (f32[81,8,512]{2,1,0:T(8,128)S(1)}, f32[81,8,512]{2,1,0:T(8,128)S(1)}, u32[]{:S(2)}, u32[]{:S(2)}) collective-permute-start(f32[81,8,512]{2,1,0:T(8,128)S(1)} %get-tuple-element.26), channel_id=1, source_target_pairs={{1,0},{2,1},{3,2},{4,3},{5,4},{6,5},{7,6},{8,7},{9,8},{10,9},{11,1... | collective-permute-start | bytes 3981320 | tf_op jit(solution)/shard_map/ppermute | solution.py:38
  97.9 27.7 %collective-permute-start.6 = (f32[4,1,256]{2,1,0:T(1,128)S(1)}, f32[4,1,256]{2,1,0:T(1,128)S(1)}, u32[]{:S(2)}, u32[]{:S(2)}) collective-permute-start(f32[4,1,256]{2,1,0:T(1,128)S(1)} %get-tuple-element.57), channel_id=1, source_target_pairs={{1,0},{2,1},{3,2},{4,3},{5,4},{6,5},{7,6},{8,7},{9,8},{10,9},{11,1... | collective-permute-start | bytes 12296 | tf_op jit(solution)/shard_map/ppermute | solution.py:19
  101.2 24.4 %collective-permute-start.7 = (f32[4,1,256]{2,1,0:T(1,128)S(1)}, f32[4,1,256]{2,1,0:T(1,128)S(1)}, u32[]{:S(2)}, u32[]{:S(2)}) collective-permute-start(f32[4,1,256]{2,1,0:T(1,128)S(1)} %get-tuple-element.58), channel_id=1, source_target_pairs={{0,1},{1,2},{2,3},{3,4},{4,5},{5,6},{6,7},{7,8},{8,9},{9,10},{10,1... | collective-permute-start | bytes 12296 | tf_op jit(solution)/shard_map/ppermute | solution.py:18
  103.3 7.2 %collective-permute-start.4 = (f32[4,32,1]{2,1,0:T(8,128)S(1)}, f32[4,32,1]{2,1,0:T(8,128)S(1)}, u32[]{:S(2)}, u32[]{:S(2)}) collective-permute-start(f32[4,32,1]{2,1,0:T(8,128)S(1)} %get-tuple-element.60), channel_id=1, source_target_pairs={{0,32},{32,64},{64,96},{1,33},{33,65},{65,97},{2,34},{34,66},{66,9... | collective-permute-start | bytes 1544 | tf_op jit(solution)/shard_map/ppermute | solution.py:18
  110.4 8.0 %collective-permute-start.5 = (f32[4,32,1]{2,1,0:T(8,128)S(1)}, f32[4,32,1]{2,1,0:T(8,128)S(1)}, u32[]{:S(2)}, u32[]{:S(2)}) collective-permute-start(f32[4,32,1]{2,1,0:T(8,128)S(1)} %get-tuple-element.59), channel_id=1, source_target_pairs={{32,0},{64,32},{96,64},{33,1},{65,33},{97,65},{34,2},{66,34},{98,6... | collective-permute-start | bytes 1544 | tf_op jit(solution)/shard_map/ppermute | solution.py:19
  125.9 90.4 %collective-permute-start.8 = (f32[4,32,1]{2,1,0:T(8,128)S(1)}, f32[4,32,1]{2,1,0:T(8,128)S(1)}, u32[]{:S(2)}, u32[]{:S(2)}) collective-permute-start(f32[4,32,1]{2,1,0:T(8,128)S(1)} %get-tuple-element.56), channel_id=1, source_target_pairs={{0,32},{32,64},{64,96},{1,33},{33,65},{65,97},{2,34},{34,66},{66,9... | collective-permute-start | bytes 1544 | tf_op jit(solution)/shard_map/ppermute | solution.py:18
  131.4 84.9 %collective-permute-start.9 = (f32[4,32,1]{2,1,0:T(8,128)S(1)}, f32[4,32,1]{2,1,0:T(8,128)S(1)}, u32[]{:S(2)}, u32[]{:S(2)}) collective-permute-start(f32[4,32,1]{2,1,0:T(8,128)S(1)} %get-tuple-element.55), channel_id=1, source_target_pairs={{32,0},{64,32},{96,64},{33,1},{65,33},{97,65},{34,2},{66,34},{98,6... | collective-permute-start | bytes 1544 | tf_op jit(solution)/shard_map/ppermute | solution.py:19
  133.3 83.0 %collective-permute-start.10 = (f32[4,1,256]{2,1,0:T(1,128)S(1)}, f32[4,1,256]{2,1,0:T(1,128)S(1)}, u32[]{:S(2)}, u32[]{:S(2)}) collective-permute-start(f32[4,1,256]{2,1,0:T(1,128)S(1)} %get-tuple-element.53), channel_id=1, source_target_pairs={{1,0},{2,1},{3,2},{4,3},{5,4},{6,5},{7,6},{8,7},{9,8},{10,9},{11,1... | collective-permute-start | bytes 12296 | tf_op jit(solution)/shard_map/ppermute | solution.py:19
  142.4 73.9 %collective-permute-start.11 = (f32[4,1,256]{2,1,0:T(1,128)S(1)}, f32[4,1,256]{2,1,0:T(1,128)S(1)}, u32[]{:S(2)}, u32[]{:S(2)}) collective-permute-start(f32[4,1,256]{2,1,0:T(1,128)S(1)} %get-tuple-element.54), channel_id=1, source_target_pairs={{0,1},{1,2},{2,3},{3,4},{4,5},{5,6},{6,7},{7,8},{8,9},{9,10},{10,1... | collective-permute-start | bytes 12296 | tf_op jit(solution)/shard_map/ppermute | solution.py:18
  145.6 35.9 %copy-start.1 = (f32[32,512]{1,0:T(8,128)}, f32[32,512]{1,0:T(8,128)S(1)}, u32[]{:S(2)}) copy-start(f32[32,512]{1,0:T(8,128)S(1)} %maximum_bitcast_fusion.2) | copy-start | bytes 196612
  187.8 16.2 %slice-start = ((f32[32,512]{1,0:T(8,128)}), f32[16,512]{1,0:T(8,128)S(1)}, s32[]{:S(2)}) async-start(f32[32,512]{1,0:T(8,128)} %copy-done.1), calls=%async_computation.2 | async-start | bytes 65536 | tf_op jit(solution)/shard_map/slice | solution.py:157
  211.7 9.6 %all-to-all-start.1 = ((f32[4,4,16,128]{3,2,1,0:T(8,128)}), f32[4,4,16,128]{3,2,1,0:T(8,128)S(1)}, u32[]{:S(2)}, u32[]{:S(2)}) async-start(f32[4,4,16,128]{3,2,1,0:T(8,128)} %copy.476), calls=%async_computation.1 | async-start | bytes 262144 | tf_op jit(solution)/shard_map/all_to_all | solution.py:65
  221.9 9.1 %collective-permute-start.22 = (f32[16,4,16,1]{3,1,2,0:T(4,128)S(1)}, f32[16,4,16,1]{3,1,2,0:T(4,128)S(1)}, u32[]{:S(2)}, u32[]{:S(2)}) collective-permute-start(f32[16,4,16,1]{3,1,2,0:T(4,128)S(1)} %get-tuple-element.45), channel_id=1, source_target_pairs={{0,32},{32,64},{64,96},{1,33},{33,65},{65,97},{2,34},{34,66},{66,9... | collective-permute-start | bytes 12296 | tf_op jit(solution)/shard_map/ppermute | solution.py:35
  224.8 12.0 %collective-permute-start.23 = (f32[16,4,16,1]{3,1,2,0:T(4,128)S(1)}, f32[16,4,16,1]{3,1,2,0:T(4,128)S(1)}, u32[]{:S(2)}, u32[]{:S(2)}) collective-permute-start(f32[16,4,16,1]{3,1,2,0:T(4,128)S(1)} %get-tuple-element.46), channel_id=1, source_target_pairs={{32,0},{64,32},{96,64},{33,1},{65,33},{97,65},{34,2},{66,34},{98,6... | collective-permute-start | bytes 12296 | tf_op jit(solution)/shard_map/ppermute | solution.py:38
  237.0 18.1 %collective-permute-start.24 = (f32[16,4,1,130]{3,1,2,0:T(4,128)S(1)}, f32[16,4,1,130]{3,1,2,0:T(4,128)S(1)}, u32[]{:S(2)}, u32[]{:S(2)}) collective-permute-start(f32[16,4,1,130]{3,1,2,0:T(4,128)S(1)} %get-tuple-element.27), channel_id=1, source_target_pairs={{0,1},{1,2},{2,3},{3,4},{4,5},{5,6},{6,7},{7,8},{8,9},{9,10},{10,1... | collective-permute-start | bytes 99848 | tf_op jit(solution)/shard_map/ppermute | solution.py:35
  238.9 18.1 %collective-permute-start.25 = (f32[16,4,1,130]{3,1,2,0:T(4,128)S(1)}, f32[16,4,1,130]{3,1,2,0:T(4,128)S(1)}, u32[]{:S(2)}, u32[]{:S(2)}) collective-permute-start(f32[16,4,1,130]{3,1,2,0:T(4,128)S(1)} %get-tuple-element.28), channel_id=1, source_target_pairs={{1,0},{2,1},{3,2},{4,3},{5,4},{6,5},{7,6},{8,7},{9,8},{10,9},{11,1... | collective-permute-start | bytes 99848 | tf_op jit(solution)/shard_map/ppermute | solution.py:38
  247.4 23.3 %collective-permute-start.12 = (f32[4,32,1]{2,1,0:T(8,128)S(1)}, f32[4,32,1]{2,1,0:T(8,128)S(1)}, u32[]{:S(2)}, u32[]{:S(2)}) collective-permute-start(f32[4,32,1]{2,1,0:T(8,128)S(1)} %get-tuple-element.52), channel_id=1, source_target_pairs={{0,32},{32,64},{64,96},{1,33},{33,65},{65,97},{2,34},{34,66},{66,9... | collective-permute-start | bytes 1544 | tf_op jit(solution)/shard_map/ppermute | solution.py:18
  249.4 21.3 %collective-permute-start.13 = (f32[4,32,1]{2,1,0:T(8,128)S(1)}, f32[4,32,1]{2,1,0:T(8,128)S(1)}, u32[]{:S(2)}, u32[]{:S(2)}) collective-permute-start(f32[4,32,1]{2,1,0:T(8,128)S(1)} %get-tuple-element.51), channel_id=1, source_target_pairs={{32,0},{64,32},{96,64},{33,1},{65,33},{97,65},{34,2},{66,34},{98,6... | collective-permute-start | bytes 1544 | tf_op jit(solution)/shard_map/ppermute | solution.py:19
  251.8 18.9 %collective-permute-start.14 = (f32[4,1,256]{2,1,0:T(1,128)S(1)}, f32[4,1,256]{2,1,0:T(1,128)S(1)}, u32[]{:S(2)}, u32[]{:S(2)}) collective-permute-start(f32[4,1,256]{2,1,0:T(1,128)S(1)} %get-tuple-element.49), channel_id=1, source_target_pairs={{1,0},{2,1},{3,2},{4,3},{5,4},{6,5},{7,6},{8,7},{9,8},{10,9},{11,1... | collective-permute-start | bytes 12296 | tf_op jit(solution)/shard_map/ppermute | solution.py:19
  255.2 15.6 %collective-permute-start.15 = (f32[4,1,256]{2,1,0:T(1,128)S(1)}, f32[4,1,256]{2,1,0:T(1,128)S(1)}, u32[]{:S(2)}, u32[]{:S(2)}) collective-permute-start(f32[4,1,256]{2,1,0:T(1,128)S(1)} %get-tuple-element.50), channel_id=1, source_target_pairs={{0,1},{1,2},{2,3},{3,4},{4,5},{5,6},{6,7},{7,8},{8,9},{9,10},{10,1... | collective-permute-start | bytes 12296 | tf_op jit(solution)/shard_map/ppermute | solution.py:18
  264.7 6.1 %copy-start.2 = (f32[4,32,256]{2,1,0:T(8,128)S(1)}, f32[4,32,256]{2,1,0:T(8,128)}, u32[]{:S(2)}) copy-start(f32[4,32,256]{2,1,0:T(8,128)} %param.8) | copy-start | bytes 393220
where the time goes:
time: 274 us; the launch traced here: 272 us
  starting transfers between devices  111 us (41%)
  local copies, waits for them, and re-layouts  68.2 us (25%)
  other arithmetic  61.9 us (23%)
  waiting for transfers between devices  30.3 us (11%)
    add x11, other arithmetic, diffuse(): return centre + rate_field * (beside - 4.0 * centre)  49.2 us
    ppermute x8, starting transfers between devices, padded_2(): lax.ppermute(first, axis, [(b, a) for a, b in up])  32.7 us
    ppermute x5, starting transfers between devices, with_halo(): lax.ppermute(lax.slice_in_dim(block, 0, width, axis=dim), axis, backward)  26.3 us
    ppermute x8, starting transfers between devices, padded_2(): lax.ppermute(last, axis, up)  26 us
    slice x1, local copies, waits for them, and re-layouts, restrict(): parity[:, row_block:row_block + height, row_parity, col_block:col_block +...  23.9 us
    slice x1, local copies, waits for them, and re-layouts, diffuse(): padded[..., 2:, 1:-1] + padded[..., :-2, 1:-1] + padded[..., 1:-1, 2:]  16.2 us
    ppermute x5, starting transfers between devices, with_halo(): lax.ppermute(lax.slice_in_dim(block, block.shape[dim] - width, None, axis...  15.1 us
    ppermute x8, waiting for transfers between devices, padded_2(): lax.ppermute(first, axis, [(b, a) for a, b in up])  13.3 us
  transfers between devices with their start and end apart: 28, of which 7 were waited for; matrix products, arithmetic and copies ran while one was open for 47% of the time, Pallas kernels for 0%

commit v1 on v0

v1 whole, which is shorter than its diff:
```python
import functools

import jax
import jax.numpy as jnp
from jax import lax
from jax.experimental import pallas as pl
from jax.experimental.pallas import tpu as pltpu
from jax.sharding import PartitionSpec as P

STATIC_PASSES = 4
SPREAD_PASSES = 8
REACH = SPREAD_PASSES // 2
FIELDS = 4
MESH = pl.DeviceIdType.MESH
F32 = jnp.float32
BF16 = jnp.bfloat16
AROUND = [(0, 1), (0, -1), (1, 0), (-1, 0), (1, 1), (1, -1), (-1, 1), (-1, -1)]
CHUNK = 4


def split_dot(x, one_hot, transposed=False):
    high = x.astype(BF16)
    rest = x - high.astype(F32)
    mid = rest.astype(BF16)
    low = (rest - mid.astype(F32)).astype(BF16)
    terms = jnp.concatenate([high, mid, low], axis=0)
    dims = (((1,), (1 if transposed else 0,)), ((), ()))
    out = lax.dot_general(terms, one_hot, dims, preferred_element_type=F32)
    n = x.shape[0]
    return (out[2 * n :] + out[n : 2 * n]) + out[:n]


def first_row(step):
    return max(-step, step - SPREAD_PASSES - REACH)


def row_chunks(low, high):
    return [(r, min(r + CHUNK - 1, high)) for r in range(low, high + 1, CHUNK)]


def beside(row, lane):
    axis = row[0].ndim - 1
    zero = jnp.zeros_like(row[0])
    left = jnp.where(lane == 0, zero, pltpu.roll(row[3], 1, axis))
    right = jnp.where(lane == 127, zero, pltpu.roll(row[0], 127, axis))
    return [left + row[1], row[0] + row[2], row[1] + row[3], row[2] + right]


def kernel(
    rate_ref, grad_hbm, scale_hbm, index_hbm, weight_hbm, members_hbm, spread_hbm, out_ref,
    grad, scale, index, weight, spread, raw, perm, pick, place,
    mbuf, edge, table, table_h, picked, coarse, coarse_e, cperm, cb, ceb, kb, ab,
    pa, pb, acc, halo_v, part, got, esum, eup, edown, eall, lhs, fine, static_buf,
    local_sem, send_sem, recv_sem,
):
    m, t = lax.axis_index("mem"), lax.axis_index("tile")
    groups, tiles = lax.axis_size("mem"), lax.axis_size("tile")
    member_count = raw.shape[0]
    mf = member_count * FIELDS
    steps = mf // 8

    def at(dm, dt):
        return (lax.rem(m + dm + groups, groups), lax.rem(t + dt + tiles, tiles))

    barrier = pltpu.get_barrier_semaphore()
    peers = AROUND + [(2, 0)]
    for dm, dt in peers:
        pl.semaphore_signal(barrier, inc=1, device_id=at(dm, dt), device_id_type=MESH)

    locals_ = []

    def fetch(src, dst):
        copy = pltpu.make_async_copy(src, dst, local_sem.at[len(locals_)])
        locals_.append(copy)
        copy.start()
        return copy

    fetch_grad = fetch(grad_hbm, grad.at[:, 8:40, 128:384])
    fetch_members = fetch(members_hbm, raw)
    fetch_index = fetch(index_hbm, index.at[:, 8:24, 128:256])
    fetch_weight = fetch(weight_hbm, weight.at[:, 8:24, 128:256])
    fetch_spread = fetch(spread_hbm, spread.at[8:24])
    fetch_scale = fetch(scale_hbm, scale.at[:, 8:40, 128:384])

    sent = []

    def send(src, dst, dm, dt):
        number = len(sent)
        copy = pltpu.make_async_remote_copy(
            src_ref=src, dst_ref=dst, send_sem=send_sem.at[number], recv_sem=recv_sem.at[number],
            device_id=at(dm, dt), device_id_type=MESH,
        )
        sent.append(copy)
        copy.start()
        return copy

    def send_rim(buf, rows, cols):
        copies = []
        for dm, dt in AROUND:
            row = {0: (8, 8, rows), 1: (rows, 0, 8), -1: (8, rows + 8, 8)}[dt]
            col = {0: (128, 128, cols), 1: (cols, 0, 128), -1: (128, cols + 128, 128)}[dm]
            copies.append(
                send(
                    buf.at[:, row[0] : row[0] + row[2], col[0] : col[0] + col[2]],
                    buf.at[:, row[1] : row[1] + row[2], col[1] : col[1] + col[2]],
                    dm, dt,
                )
            )
        return copies

    def wait_all(copies):
        for copy in copies:
            copy.wait_recv()

    source = lax.broadcasted_iota(jnp.int32, (512, 512), 0)
    target = lax.broadcasted_iota(jnp.int32, (512, 512), 1)
    perm[...] = (source == 4 * (target & 127) + (target >> 7)).astype(F32).astype(BF16)

    fetch_grad.wait()
    fetch_spread.wait()
    pl.semaphore_wait(barrier, len(peers))
    rim_grad = send_rim(grad, 32, 256)
    rim_spread = [
        send(spread.at[16:24], spread.at[0:8], 0, 1),
        send(spread.at[8:16], spread.at[24:32], 0, -1),
    ]

    fetch_members.wait()

    def convert(i, carry):
        block = raw[pl.ds(2 * i, 2)].reshape(8 * 16, 512)
        out = jnp.dot(block, perm[...], preferred_element_type=F32)
        for q in range(8):
            for j in range(4):
                mbuf[j, pl.ds(8 * i + q, 16, stride=mf), :] = out[
                    16 * q : 16 * q + 16, 128 * j : 128 * j + 128
                ]
        return carry

    lax.fori_loop(0, steps, convert, 0)
    edge_members = [
        send(mbuf.at[:, 12 * mf : 16 * mf], edge.at[0], 0, 1),
        send(mbuf.at[:, 0 : 4 * mf], edge.at[1], 0, -1),
    ]

    fetch_index.wait()
    fetch_weight.wait()
    for o in range(16):
        total = jnp.zeros((16, 128), F32)
        for s in range(4):
            total = total + jnp.where(index[s, 8:24, 128:256] == o, weight[s, 8:24, 128:256], 0.0)
        table[o, 8:24] = total
    source = lax.broadcasted_iota(jnp.int32, (384, 512), 0)
    target = lax.broadcasted_iota(jnp.int32, (384, 512), 1)
    wanted = 2 * (target & 127) + (target >> 7) - 1
    wanted = jnp.where(wanted < 0, 383, wanted)
    pick[...] = (source == wanted).astype(F32).astype(BF16)
    source = lax.broadcasted_iota(jnp.int32, (640, 256), 0)
    target = lax.broadcasted_iota(jnp.int32, (640, 256), 1)
    inner = (source < 512) & (target == 2 * (source & 127) + (source >> 7) - 1)
    left = (source == 639) & (target == 0)
    right = (source == 512) & (target == 255)
    place[...] = (inner | left | right).astype(F32).astype(BF16)

    rows48 = lax.broadcasted_iota(jnp.int32, (48, 384), 0)
    lanes48 = lax.broadcasted_iota(jnp.int32, (48, 384), 1)
    inside = (t > 0) | (rows48 >= 8)
    inside = inside & ((t < tiles - 1) | (rows48 < 40))
    inside = inside & ((m > 0) | (lanes48 < 320))
    inside = inside & ((m < groups - 1) | (lanes48 < 256) | (lanes48 >= 320))
    lane48 = lax.broadcasted_iota(jnp.int32, (48, 128), 1)

    def rimmed(buf, f):
        rim = jnp.where(lane48 < 64, buf[f, :, 384:512], buf[f, :, 0:128])
        return jnp.concatenate([buf[f, :, 128:384], rim], axis=1)

    wait_all(rim_grad)
    padded = jnp.concatenate(
        [jnp.where(inside, rimmed(grad, f), 0.0) for f in range(FIELDS)], axis=0
    )
    out = split_dot(padded, pick[...])
    for b in range(4):
        picked[b] = out[:, 128 * b : 128 * b + 128]
    for f in range(FIELDS):
        total = jnp.zeros((16, 128), F32)
        for a in range(4):
            for b in range(4):
                total = total + table[4 * a + b, 8:24] * picked[
                    b, pl.ds(48 * f + 7 + a, 16, stride=2), :
                ]
        coarse[m, f] = total
    all_coarse = [send(coarse.at[m], coarse.at[m], o, 0) for o in (1, 2, 3)]

    wait_all(rim_spread)
    out = split_dot(spread[...], perm[...])
    row32 = lax.broadcasted_iota(jnp.int32, (32, 512), 0)
    known = ((t > 0) | (row32 >= 8)) & ((t < tiles - 1) | (row32 < 24))
    rate = jnp.where(known, out, 0.0)
    stay = jnp.where(known, 1.0 - 4.0 * out, 0.0)
    for j in range(4):
        for r in range(1, 31):
            kb[j, r] = jnp.broadcast_to(rate[r : r + 1, 128 * j : 128 * j + 128], (8, 128))
            ab[j, r] = jnp.broadcast_to(stay[r : r + 1, 128 * j : 128 * j + 128], (8, 128))
    acc[...] = jnp.zeros_like(acc)

    wait_all(all_coarse)
    edge_coarse = [
        send(coarse.at[:, :, 8:16], coarse_e.at[0], 0, 1),
        send(coarse.at[:, :, 0:8], coarse_e.at[1], 0, -1),
    ]
    fetch_scale.wait()
    rim_scale = send_rim(scale, 32, 256)
    rim_index = send_rim(index, 16, 128)
    rim_weight = send_rim(weight, 16, 128)

    rows = jnp.concatenate([coarse[q].reshape(64, 128) for q in range(4)], axis=1)
    out = split_dot(rows, perm[...])
    for j in range(4):
        cperm[j, 0:64] = out[:, 128 * j : 128 * j + 128]
    for j in range(4):
        for r in range(16):
            four = cperm[j, pl.ds(r, 4, stride=16), :]
            cb[j, r, 0:4] = four
            cb[j, r, 4:8] = four

    zero2 = jnp.zeros((2, 8, 128), F32)

    def spread_own(g, carry):
        bufs = [pa, pb]
        for j in range(4):
            for r in range(16):
                pa[j, r + 8] = mbuf[j, pl.ds(r * mf + 8 * g, 8), :] * cb[j, r]
            pa[j, 6:8] = zero2
            pa[j, 24:26] = zero2
        for step in range(1, SPREAD_PASSES + 1):
            src, dst = bufs[(step - 1) % 2], bufs[step % 2]
            low = first_row(step)
            high = 15 - low
            if step <= 6:
                for j in range(4):
                    dst[j, low + 6 : low + 8] = zero2
                    dst[j, high + 9 : high + 11] = zero2
            last = step == SPREAD_PASSES
            if last:
                pieces = row_chunks(-REACH, -1) + row_chunks(0, 15) + row_chunks(16, 15 + REACH)
            else:
                pieces = row_chunks(low, high)
            for r0, r1 in pieces:
                n = r1 - r0 + 1
                lane = lax.broadcasted_iota(jnp.int32, (n, 8, 128), 2)
                x = [src[j, r0 + 7 : r1 + 10] for j in range(4)]
                centre = [v[1 : n + 1] for v in x]
                sides = beside(centre, lane)
                for j in range(4):
                    around = (x[j][0:n] + x[j][2 : n + 2]) + sides[j]
                    new = ab[j, r0 + 8 : r1 + 9] * centre[j] + kb[j, r0 + 8 : r1 + 9] * around
                    if not last:
                        dst[j, r0 + 8 : r1 + 9] = new
                    elif r0 < 0:
                        halo_v[g, j, r0 + 4 : r1 + 5] = new
                    elif r0 >= 16:
                        halo_v[g, j, r0 - 12 : r1 - 11] = new
                    else:
                        for r in range(r0, r1 + 1):
                            acc[j, r + 4] += new[r - r0] * mbuf[j, pl.ds(r * mf + 8 * g, 8), :]
        return carry

    lax.fori_loop(0, steps, spread_own, 0)

    wait_all(edge_coarse)
    rows = jnp.concatenate(
        [
            jnp.concatenate([coarse_e[side, q].reshape(32, 128) for q in range(4)], axis=1)
            for side in range(2)
        ],
        axis=0,
    )
    out = split_dot(rows, perm[...])
    for j in range(4):
        cperm[j, 0:64] = out[:, 128 * j : 128 * j + 128]
    for side in range(2):
        there = (t > 0) if side == 0 else (t < tiles - 1)
        for j in range(4):
            for r in range(4):
                start = 32 * side + (4 + r if side == 0 else r)
                four = jnp.where(there, cperm[j, pl.ds(start, 4, stride=8), :], 0.0)
                ceb[side, j, r, 0:4] = four
                ceb[side, j, r, 4:8] = four
    wait_all(edge_members)

    lane8 = lax.broadcasted_iota(jnp.int32, (8, 128), 1)

    def spread_edges(g, carry):
        for side in range(2):
            old = []
            for r in range(4):
                row = []
                for j in range(4):
                    theirs = edge[side, j, pl.ds(r * mf + 8 * g, 8), :]
                    to = r if side == 0 else 20 + r
                    acc[j, to] += theirs * halo_v[g, j, 4 * side + r]
                    row.append(theirs * ceb[side, j, r])
                old.append(row)
            for step in range(1, SPREAD_PASSES + 1):
                base = 8 + (step - REACH if side == 0 else 16 - step)
                shift = 1 if side == 0 else -1
                nxt = []
                for i in range(4):
                    terms = [old[i + shift + d] for d in (-1, 1) if 0 <= i + shift + d < 4]
                    row = []
                    same = old[i + shift] if 0 <= i + shift < 4 else None
                    sides = beside(same, lane8) if same is not None else None
                    for j in range(4):
                        parts = [term[j] for term in terms]
                        if sides is not None:
                            parts.append(sides[j])
                        around = functools.reduce(lambda a, b: a + b, parts)
                        new = kb[j, base + i] * around
                        if same is not None:
                            new = ab[j, base + i] * same[j] + new
                        row.append(new)
                    nxt.append(row)
                old = nxt
            for i in range(4):
                r = i + (4 if side == 0 else 8)
                for j in range(4):
                    acc[j, r + 4] += old[i][j] * mbuf[j, pl.ds(r * mf + 8 * g, 8), :]
        return carry

    lax.fori_loop(0, steps, spread_edges, 0)

    sub = lax.broadcasted_iota(jnp.int32, (12, 8, 128), 1)
    folded = []
    for j in range(4):
        x = acc[j]
        y = (x + pltpu.roll(x, 4, 1)).reshape(12, 2, 8, 128)
        folded.append(jnp.where(sub < 4, y[:, 0], y[:, 1]).reshape(96, 128))
    out = split_dot(jnp.concatenate(folded, axis=1), perm[...], transposed=True)
    for q in range(4):
        part[q] = out[:, 128 * q : 128 * q + 128]
    shares = [
        send(part.at[lax.rem(m + o, groups)], got.at[o - 1], o, 0) for o in (1, 2, 3)
    ]

    wait_all(rim_index)
    wait_all(rim_weight)
    row8 = lax.broadcasted_iota(jnp.int32, (32, 128), 0)
    lane32 = lax.broadcasted_iota(jnp.int32, (32, 128), 1)
    in_rows = ((t > 0) | (row8 >= 8)) & ((t < tiles - 1) | (row8 < 24))
    in_cols = jnp.where(lane32 < 64, (m < groups - 1).astype(jnp.int32), (m > 0).astype(jnp.int32))
    in_rim = in_rows & (in_cols > 0)
    for a in range(4):
        total = jnp.zeros((32, 128), F32)
        for s in range(4):
            near = jnp.where(lane32 < 64, index[s, :, 256:384], index[s, :, 0:128])
            amount = jnp.where(lane32 < 64, weight[s, :, 256:384], weight[s, :, 0:128])
            cell = jnp.where(lane32 < 64, 4 * a, 4 * a + 3)
            total = total + jnp.where(near == cell, amount, 0.0)
        table_h[a] = jnp.where(in_rim, total, 0.0)
    for b in range(4):
        top = jnp.zeros((8, 128), F32)
        bottom = jnp.zeros((8, 128), F32)
        for s in range(4):
            top = top + jnp.where(index[s, 0:8, 128:256] == 12 + b, weight[s, 0:8, 128:256], 0.0)
            bottom = bottom + jnp.where(
                index[s, 24:32, 128:256] == b, weight[s, 24:32, 128:256], 0.0
            )
        table[12 + b, 0:8] = jnp.where(t > 0, top, 0.0)
        table[b, 24:32] = jnp.where(t < tiles - 1, bottom, 0.0)

    wait_all(rim_scale)
    for f in range(FIELDS):
        p = jnp.where(inside, rimmed(scale, f) * rimmed(grad, f), 0.0)
        for _ in range(STATIC_PASSES):
            around = (pltpu.roll(p, 1, 0) + pltpu.roll(p, 47, 0)) + (
                pltpu.roll(p, 1, 1) + pltpu.roll(p, 383, 1)
            )
            p = jnp.where(inside, p + rate_ref[f] * (around - 4.0 * p), 0.0)
        static_buf[f] = scale[f, 8:40, 128:384] * p[8:40, 0:256]

    wait_all(shares)
    esum[1] = (part[m] + got[0]) + (got[1] + got[2])
    rims = []
    for dm, dt in AROUND:
        slot = 1 - dm
        if dt == 0:
            rims.append(send(esum.at[1], esum.at[slot], dm, dt))
        elif dt == 1:
            rims.append(send(esum.at[1, 72:96], eup.at[slot], dm, dt))
        else:
            rims.append(send(esum.at[1, 0:24], edown.at[slot], dm, dt))
    wait_all(rims)
    members_all = member_count * groups

    def whole(slot):
        eall[slot] = esum[slot]
        eall[slot, 8:32] += eup[slot]
        eall[slot, 64:88] += edown[slot]

    for slot in range(3):
        whole(slot)
    lane96 = lax.broadcasted_iota(jnp.int32, (96, 128), 1)
    side_e = jnp.where(lane96 < 64, eall[2], eall[0]) / (members_all - 1)
    eall[1] = eall[1] / (members_all - 1)
    eall[0] = side_e
    for parity in range(2):
        pairs = [(1, 0), (3, -1)] if parity == 0 else [(2, 0), (0, 1)]
        for f in range(FIELDS):
            at_row = 16 * (4 * parity + f)
            mids = [eall[1, pl.ds(4 * (4 + d) + f, 16, stride=4), :] for _, d in pairs]
            ends = [eall[0, pl.ds(4 * (4 + d) + f, 16, stride=4), :] for _, d in pairs]
            for b in range(4):
                lhs[at_row : at_row + 16, 128 * b : 128 * b + 128] = (
                    table[4 * pairs[0][0] + b, 8:24] * mids[0]
                    + table[4 * pairs[1][0] + b, 8 + pairs[1][1] : 24 + pairs[1][1]] * mids[1]
                )
            lhs[at_row : at_row + 16, 512:640] = (
                table_h[pairs[0][0], 8:24] * ends[0]
                + table_h[pairs[1][0], 8 + pairs[1][1] : 24 + pairs[1][1]] * ends[1]
            )
    out = split_dot(lhs[...], place[...])
    for parity in range(2):
        for f in range(FIELDS):
            at_row = 16 * (4 * parity + f)
            for x in range(2):
                fine[x, pl.ds(32 * f + parity, 16, stride=2), :] = out[
                    at_row : at_row + 16, 128 * x : 128 * x + 128
                ]
    for f in range(FIELDS):
        for x in range(2):
            cols = slice(128 * x, 128 * x + 128)
            out_ref[f, :, cols] = 0.3 * static_buf[f, :, cols] + 2.8 * fine[x, 32 * f : 32 * f + 32]
    for copy in sent:
        copy.wait_send()


def local(gradient, static_scale, static_rate, interp_index, interp_weight, members, spread_rate):
    member_count = members.shape[0]
    mf = member_count * FIELDS
    anywhere = pl.BlockSpec(memory_space=pl.ANY)
    vmem = pltpu.VMEM
    sems = 64
    return pl.pallas_call(
        kernel,
        out_shape=jax.ShapeDtypeStruct(gradient.shape, F32),
        in_specs=[pl.BlockSpec(memory_space=pltpu.SMEM)] + [anywhere] * 6,
        out_specs=pl.BlockSpec(memory_space=pltpu.VMEM),
        scratch_shapes=[
            vmem((4, 48, 512), F32),
            vmem((4, 48, 512), F32),
            vmem((4, 32, 384), jnp.int32),
            vmem((4, 32, 384), F32),
            vmem((32, 512), F32),
            vmem(members.shape, BF16),
            vmem((512, 512), BF16),
            vmem((384, 512), BF16),
            vmem((640, 256), BF16),
            vmem((4, 16 * mf, 128), F32),
            vmem((2, 4, 4 * mf, 128), F32),
            vmem((16, 32, 128), F32),
            vmem((4, 32, 128), F32),
            vmem((4, 192, 128), F32),
            vmem((4, 4, 16, 128), F32),
            vmem((2, 4, 4, 8, 128), F32),
            vmem((4, 64, 128), F32),
            vmem((4, 16, 8, 128), F32),
            vmem((2, 4, 4, 8, 128), F32),
            vmem((4, 32, 8, 128), F32),
            vmem((4, 32, 8, 128), F32),
            vmem((4, 32, 8, 128), F32),
            vmem((4, 32, 8, 128), F32),
            vmem((4, 24, 8, 128), F32),
            vmem((mf // 8, 4, 8, 8, 128), F32),
            vmem((4, 96, 128), F32),
            vmem((3, 96, 128), F32),
            vmem((3, 96, 128), F32),
            vmem((3, 24, 128), F32),
            vmem((3, 24, 128), F32),
            vmem((3, 96, 128), F32),
            vmem((128, 640), F32),
            vmem((2, 128, 128), F32),
            vmem((4, 32, 256), F32),
            pltpu.SemaphoreType.DMA((6,)),
            pltpu.SemaphoreType.DMA((sems,)),
            pltpu.SemaphoreType.DMA((sems,)),
        ],
        compiler_params=pltpu.CompilerParams(
            collective_id=0, has_side_effects=True, vmem_limit_bytes=56 << 20
        ),
    )(static_rate, gradient, static_scale, interp_index, interp_weight, members, spread_rate)


def solution(mesh):
    return jax.shard_map(
        local,
        mesh=mesh,
        in_specs=(
            P(None, "tile", "mem"),
            P(None, "tile", "mem"),
            P(),
            P(None, "tile", "mem"),
            P(None, "tile", "mem"),
            P("mem", None, "tile", None),
            P("tile", None),
        ),
        out_specs=P(None, "tile", "mem"),
        check_vma=False,
    )
```

time: 274 us -> 60.5 us (0.22)
  the two profiles are of different devices: /device:TPU:33 before, /device:TPU:1 now
where the time goes in v1:
time: 60.5 us; the launch traced here: 60.4 us
  Pallas kernels  58.8 us (97%)
  local copies, waits for them, and re-layouts  1.57 us (3%)
    pallas_call x1, Pallas kernels, local(): pl.pallas_call(kernel, out_shape=jax.ShapeDtypeStruct(gradient.shape, F32...  58.8 us
    unnamed x1, local copies, waits for them, and re-layouts  1.57 us

profile of v1, /device:TPU:1, one launch (start us, length us, event | category | flops | bytes accessed | tf_op | source)
XLA Modules:
  0.0 60.4 jit_solution(12624274444890728213)
XLA Ops:
  0.0 58.8 %shard_map.73 = f32[4,32,256]{2,1,0:T(8,128)} custom-call(f32[4]{0:T(128)} %rate_ref.1, f32[4,32,256]{2,1,0:T(8,128)} %grad_hbm.1, f32[4,32,256]{2,1,0:T(8,128)} %scale_hbm.1, s32[4,16,128]{2,1,0:T(8,128)} %index_hbm.1, f32[4,16,128]{2,1,0:T(8,128)} %weight_hbm.1, bf16[20,4,16,512]{3,2,1,0:T(8,128)(2,1)} %members_hbm.1, f32[16,512]{1,0:T(8,128)} %spread_hbm.1), custom_call_target="tpu_custom_call" | custom-call | tf_op jit(solution)/shard_map/pallas_call | solution.py:443
  58.8 1.6 %copy.9 = f32[4,32,256]{2,1,0:T(8,128)} copy(f32[4,32,256]{2,1,0:T(8,128)} %shard_map.73) | data formatting | bytes 262144

commit v2 on v1

--- a/solution.py
+++ b/solution.py
@@ -16,6 +16,7 @@
 BF16 = jnp.bfloat16
 AROUND = [(0, 1), (0, -1), (1, 0), (-1, 0), (1, 1), (1, -1), (-1, 1), (-1, -1)]
 CHUNK = 4
+ZROW = 16
 
 
 def split_dot(x, one_hot, transposed=False):
@@ -48,8 +49,9 @@
 
 def kernel(
     rate_ref, grad_hbm, scale_hbm, index_hbm, weight_hbm, members_hbm, spread_hbm, out_ref,
-    grad, scale, index, weight, spread, raw, perm, pick, place,
-    mbuf, edge, table, table_h, picked, coarse, coarse_e, cperm, cb, ceb, kb, ab,
+    grad, scale, grad_out, grad_in, scale_out, scale_in, index, weight,
+    table_col, table_col_in, table_row, table_row_in, spread, raw, perm, pick, place,
+    mbuf, edge, passing, table, table_h, picked, coarse, coarse_e, cperm, cb, ceb, kb, ab,
     pa, pb, acc, halo_v, part, got, esum, eup, edown, eall, lhs, fine, static_buf,
     local_sem, send_sem, recv_sem,
 ):
@@ -62,10 +64,44 @@
     def at(dm, dt):
         return (lax.rem(m + dm + groups, groups), lax.rem(t + dt + tiles, tiles))
 
+    def there(dm, dt):
+        tests = []
+        if dm:
+            tests.append(m < groups - 1 if dm > 0 else m > 0)
+        if dt:
+            tests.append(t < tiles - 1 if dt > 0 else t > 0)
+        return functools.reduce(jnp.logical_and, tests) if tests else None
+
+    def only(test, action):
+        if test is None:
+            action()
+        else:
+            pl.when(test)(action)
+
     barrier = pltpu.get_barrier_semaphore()
-    peers = AROUND + [(2, 0)]
-    for dm, dt in peers:
+
+    def greet(dm, dt):
         pl.semaphore_signal(barrier, inc=1, device_id=at(dm, dt), device_id_type=MESH)
+
+    waited = 3
+    for o in (1, 2, 3):
+        greet(o, 0)
+    for dm, dt in AROUND:
+        if dt:
+            only(there(dm, dt), functools.partial(greet, dm, dt))
+            waited = waited + there(dm, dt).astype(jnp.int32)
+    up_end, down_end = lax.rem(t, ZROW) == ZROW - 1, lax.rem(t, ZROW) == 0
+    feeder = (up_end & (t < tiles - 1)) | (down_end & (t > 0))
+    relay = (up_end | down_end) & ~feeder
+    over = jnp.where(t < ZROW, ZROW, -ZROW)
+    along = jnp.where(up_end, 1 - ZROW, ZROW - 1)
+
+    @pl.when(up_end | down_end)
+    def _():
+        greet(0, over)
+        greet(0, along)
+
+    waited = waited + 2 * (up_end | down_end).astype(jnp.int32)
 
     locals_ = []
 
@@ -77,79 +113,135 @@
 
     fetch_grad = fetch(grad_hbm, grad.at[:, 8:40, 128:384])
     fetch_members = fetch(members_hbm, raw)
-    fetch_index = fetch(index_hbm, index.at[:, 8:24, 128:256])
-    fetch_weight = fetch(weight_hbm, weight.at[:, 8:24, 128:256])
+    fetch_index = fetch(index_hbm, index)
+    fetch_weight = fetch(weight_hbm, weight)
     fetch_spread = fetch(spread_hbm, spread.at[8:24])
     fetch_scale = fetch(scale_hbm, scale.at[:, 8:40, 128:384])
 
     sent = []
 
-    def send(src, dst, dm, dt):
+    def send(src, dst, dm, dt, going=None, coming=None, start=True):
         number = len(sent)
         copy = pltpu.make_async_remote_copy(
             src_ref=src, dst_ref=dst, send_sem=send_sem.at[number], recv_sem=recv_sem.at[number],
             device_id=at(dm, dt), device_id_type=MESH,
         )
-        sent.append(copy)
-        copy.start()
-        return copy
-
-    def send_rim(buf, rows, cols):
+        entry = (copy, going, coming)
+        sent.append(entry)
+        if start:
+            only(entry[1], copy.start)
+        return entry
+
+    def send_near(src, dst, dm, dt):
+        return send(src, dst, dm, dt, there(dm, dt), there(-dm, -dt))
+
+    def pack(buf, out):
+        for f in range(FIELDS):
+            out[0, 4 * f : 4 * f + 4] = buf[f, 8:12, 128:384]
+            out[1, 4 * f : 4 * f + 4] = buf[f, 36:40, 128:384]
+
+    def send_rim(buf, out, come):
         copies = []
         for dm, dt in AROUND:
-            row = {0: (8, 8, rows), 1: (rows, 0, 8), -1: (8, rows + 8, 8)}[dt]
-            col = {0: (128, 128, cols), 1: (cols, 0, 128), -1: (128, cols + 128, 128)}[dm]
-            copies.append(
-                send(
-                    buf.at[:, row[0] : row[0] + row[2], col[0] : col[0] + col[2]],
-                    buf.at[:, row[1] : row[1] + row[2], col[1] : col[1] + col[2]],
-                    dm, dt,
-                )
-            )
+            col = {0: (128, 128, 256), 1: (256, 0, 128), -1: (128, 384, 128)}[dm]
+            here, land = pl.ds(col[0], col[2]), pl.ds(col[1], col[2])
+            if dt == 0:
+                src, dst = buf.at[:, 8:40, here], buf.at[:, 8:40, land]
+            else:
+                side = 1 if dt > 0 else 0
+                src = out.at[side, :, pl.ds(col[0] - 128, col[2])]
+                dst = come.at[1 - side, :, land]
+            copies.append(send_near(src, dst, dm, dt))
         return copies
 
+    def unpack(come, buf):
+        for f in range(FIELDS):
+            buf[f, 4:8] = come[0, 4 * f : 4 * f + 4]
+            buf[f, 40:44] = come[1, 4 * f : 4 * f + 4]
+
     def wait_all(copies):
-        for copy in copies:
-            copy.wait_recv()
+        for copy, _, coming in copies:
+            only(coming, copy.wait_recv)
 
     source = lax.broadcasted_iota(jnp.int32, (512, 512), 0)
     target = lax.broadcasted_iota(jnp.int32, (512, 512), 1)
     perm[...] = (source == 4 * (target & 127) + (target >> 7)).astype(F32).astype(BF16)
 
     fetch_grad.wait()
+    pack(grad, grad_out)
     fetch_spread.wait()
-    pl.semaphore_wait(barrier, len(peers))
-    rim_grad = send_rim(grad, 32, 256)
+    pl.semaphore_wait(barrier, waited)
+    rim_grad = send_rim(grad, grad_out, grad_in)
     rim_spread = [
-        send(spread.at[16:24], spread.at[0:8], 0, 1),
-        send(spread.at[8:16], spread.at[24:32], 0, -1),
+        send_near(spread.at[16:24], spread.at[0:8], 0, 1),
+        send_near(spread.at[8:16], spread.at[24:32], 0, -1),
     ]
 
     fetch_members.wait()
 
-    def convert(i, carry):
-        block = raw[pl.ds(2 * i, 2)].reshape(8 * 16, 512)
-        out = jnp.dot(block, perm[...], preferred_element_type=F32)
-        for q in range(8):
-            for j in range(4):
-                mbuf[j, pl.ds(8 * i + q, 16, stride=mf), :] = out[
-                    16 * q : 16 * q + 16, 128 * j : 128 * j + 128
-                ]
-        return carry
-
-    lax.fori_loop(0, steps, convert, 0)
-    edge_members = [
-        send(mbuf.at[:, 12 * mf : 16 * mf], edge.at[0], 0, 1),
-        send(mbuf.at[:, 0 : 4 * mf], edge.at[1], 0, -1),
-    ]
+    half = member_count // 2
+
+    def convert(i):
+        block = raw[half * i : half * i + half].reshape(half * FIELDS * 16, 512)
+        for j in range(0, 4, 2):
+            out = jnp.dot(
+                block, perm[:, 128 * j : 128 * j + 256], preferred_element_type=F32
+            )
+            for q in range(half * FIELDS):
+                for k in range(2):
+                    mbuf[j + k, pl.ds(half * FIELDS * i + q, 16, stride=mf), :] = out[
+                        16 * q : 16 * q + 16, 128 * k : 128 * k + 128
+                    ]
+
+    convert(0)
+    convert(1)
+    edge_members, late = [[], []], []
+    for rows in (range(0, 1), range(1, 2), range(2, 4)):
+        first, count = rows[0] * mf, len(rows) * mf
+        for side, dt, cross, crossed in ((0, 1, up_end, down_end), (1, -1, down_end, up_end)):
+            here = pl.ds(first + (12 * mf if side == 0 else 0), count)
+            going, coming = there(0, dt), there(0, -dt)
+            if rows[0] < 2:
+                going, coming = going & ~cross, coming & ~crossed
+            entry = send(
+                mbuf.at[:, here], edge.at[side, :, pl.ds(first, count)], 0, dt, going, coming,
+                start=False,
+            )
+            edge_members[side].append(entry)
+            only(going & ~cross, entry[0].start)
+            if rows[0] == 2:
+                late.append((going & cross, entry[0]))
+    origin = jnp.where(up_end, 12 * mf, 0)
+    over_z, onward = [], []
+    for row in range(2):
+        from_row = pl.ds(pl.multiple_of(origin + row * mf, mf), mf)
+        over_z.append(
+            send(mbuf.at[:, from_row], passing.at[row], 0, over, feeder, relay, start=row == 0)
+        )
+        onward.append(
+            send(
+                passing.at[row],
+                edge.at[down_end.astype(jnp.int32), :, pl.ds(row * mf, mf)],
+                0, along, relay, feeder, start=False,
+            )
+        )
+    late.append((feeder, over_z[1][0]))
 
     fetch_index.wait()
     fetch_weight.wait()
     for o in range(16):
         total = jnp.zeros((16, 128), F32)
         for s in range(4):
-            total = total + jnp.where(index[s, 8:24, 128:256] == o, weight[s, 8:24, 128:256], 0.0)
+            total = total + jnp.where(index[s] == o, weight[s], 0.0)
         table[o, 8:24] = total
+        if o % 4 in (0, 3):
+            table_col[o % 4 // 3, o // 4] = total
+        if o < 4:
+            table_row[0, o : o + 1] = total[0:1]
+        if o >= 12:
+            table_row[1, o - 12 : o - 11] = total[15:16]
+    fetch_scale.wait()
+    pack(scale, scale_out)
     source = lax.broadcasted_iota(jnp.int32, (384, 512), 0)
     target = lax.broadcasted_iota(jnp.int32, (384, 512), 1)
     wanted = 2 * (target & 127) + (target >> 7) - 1
@@ -175,6 +267,7 @@
         return jnp.concatenate([buf[f, :, 128:384], rim], axis=1)
 
     wait_all(rim_grad)
+    unpack(grad_in, grad)
     padded = jnp.concatenate(
         [jnp.where(inside, rimmed(grad, f), 0.0) for f in range(FIELDS)], axis=0
     )
@@ -190,6 +283,8 @@
                 ]
         coarse[m, f] = total
     all_coarse = [send(coarse.at[m], coarse.at[m], o, 0) for o in (1, 2, 3)]
+    for test, copy in late:
+        only(test, copy.start)
 
     wait_all(rim_spread)
     out = split_dot(spread[...], perm[...])
@@ -203,15 +298,44 @@
             ab[j, r] = jnp.broadcast_to(stay[r : r + 1, 128 * j : 128 * j + 128], (8, 128))
     acc[...] = jnp.zeros_like(acc)
 
+    for side, dt in ((0, -1), (1, 1)):
+        @pl.when(jnp.logical_not(there(0, dt)))
+        def _():
+            edge[side] = jnp.zeros_like(edge[side])
+
+    for slot in range(3):
+        for dt in (-1, 0, 1):
+            if slot == 1 and dt == 0:
+                continue
+            dst = {-1: eup, 0: esum, 1: edown}[dt]
+
+            @pl.when(jnp.logical_not(there(slot - 1, dt)))
+            def _():
+                dst[slot] = jnp.zeros_like(dst[slot])
+
+    def pass_on(row):
+        @pl.when(relay)
+        def _():
+            over_z[row][0].wait_recv()
+            onward[row][0].start()
+
     wait_all(all_coarse)
+    pass_on(0)
     edge_coarse = [
-        send(coarse.at[:, :, 8:16], coarse_e.at[0], 0, 1),
-        send(coarse.at[:, :, 0:8], coarse_e.at[1], 0, -1),
+        send_near(coarse.at[:, :, 8:16], coarse_e.at[0], 0, 1),
+        send_near(coarse.at[:, :, 0:8], coarse_e.at[1], 0, -1),
     ]
-    fetch_scale.wait()
-    rim_scale = send_rim(scale, 32, 256)
-    rim_index = send_rim(index, 16, 128)
-    rim_weight = send_rim(weight, 16, 128)
+    rim_scale = send_rim(scale, scale_out, scale_in)
+    rim_table = []
+    for dm, dt in AROUND:
+        if dt == 0:
+            side = 1 if dm > 0 else 0
+            rim_table.append(send_near(table_col.at[side], table_col_in.at[1 - side], dm, dt))
+        else:
+            side = 1 if dt > 0 else 0
+            rim_table.append(
+                send_near(table_row.at[side], table_row_in.at[1 - side, 1 - dm], dm, dt)
+            )
 
     rows = jnp.concatenate([coarse[q].reshape(64, 128) for q in range(4)], axis=1)
     out = split_dot(rows, perm[...])
@@ -226,6 +350,10 @@
     zero2 = jnp.zeros((2, 8, 128), F32)
 
     def spread_own(g, carry):
+        @pl.when(g == steps // 2)
+        def _():
+            pass_on(1)
+
         bufs = [pa, pb]
         for j in range(4):
             for r in range(16):
@@ -279,55 +407,75 @@
     for j in range(4):
         cperm[j, 0:64] = out[:, 128 * j : 128 * j + 128]
     for side in range(2):
-        there = (t > 0) if side == 0 else (t < tiles - 1)
+        known = (t > 0) if side == 0 else (t < tiles - 1)
         for j in range(4):
             for r in range(4):
                 start = 32 * side + (4 + r if side == 0 else r)
-                four = jnp.where(there, cperm[j, pl.ds(start, 4, stride=8), :], 0.0)
+                four = jnp.where(known, cperm[j, pl.ds(start, 4, stride=8), :], 0.0)
                 ceb[side, j, r, 0:4] = four
                 ceb[side, j, r, 4:8] = four
-    wait_all(edge_members)
-
     lane8 = lax.broadcasted_iota(jnp.int32, (8, 128), 1)
 
-    def spread_edges(g, carry):
-        for side in range(2):
-            old = []
+    def spread_edge(side):
+        wait_all(edge_members[side])
+        only(down_end & feeder if side == 0 else up_end & feeder, onward[0][0].wait_recv)
+        only(down_end & feeder if side == 0 else up_end & feeder, onward[1][0].wait_recv)
+
+        def advance(old, step):
+            base = 8 + (step - REACH if side == 0 else 16 - step)
+            shift = 1 if side == 0 else -1
+            nxt = []
+            for i in range(4):
+                terms = [old[i + shift + d] for d in (-1, 1) if 0 <= i + shift + d < 4]
+                row = []
+                same = old[i + shift] if 0 <= i + shift < 4 else None
+                sides = beside(same, lane8) if same is not None else None
+                for j in range(4):
+                    parts = [term[j] for term in terms]
+                    if sides is not None:
+                        parts.append(sides[j])
+                    around = functools.reduce(lambda a, b: a + b, parts)
+                    new = kb[j, base + i] * around
+                    if same is not None:
+                        new = ab[j, base + i] * same[j] + new
+                    row.append(new)
+                nxt.append(row)
+            return nxt
+
+        together = 2 if steps % 2 == 0 else 1
+
+        def some(i, carry):
+            groups_ = [together * i + k for k in range(together)]
+            fields = []
             for r in range(4):
-                row = []
                 for j in range(4):
-                    theirs = edge[side, j, pl.ds(r * mf + 8 * g, 8), :]
                     to = r if side == 0 else 20 + r
-                    acc[j, to] += theirs * halo_v[g, j, 4 * side + r]
-                    row.append(theirs * ceb[side, j, r])
-                old.append(row)
+                    total = acc[j, to]
+                    for k, g in enumerate(groups_):
+                        theirs = edge[side, j, pl.ds(r * mf + 8 * g, 8), :]
+                        total = total + theirs * halo_v[g, j, 4 * side + r]
+                        fields.append(theirs * ceb[side, j, r])
+                    acc[j, to] = total
+            olds = [
+                [[fields[(4 * r + j) * together + k] for j in range(4)] for r in range(4)]
+                for k in range(together)
+            ]
             for step in range(1, SPREAD_PASSES + 1):
-                base = 8 + (step - REACH if side == 0 else 16 - step)
-                shift = 1 if side == 0 else -1
-                nxt = []
-                for i in range(4):
-                    terms = [old[i + shift + d] for d in (-1, 1) if 0 <= i + shift + d < 4]
-                    row = []
-                    same = old[i + shift] if 0 <= i + shift < 4 else None
-                    sides = beside(same, lane8) if same is not None else None
-                    for j in range(4):
-                        parts = [term[j] for term in terms]
-                        if sides is not None:
-                            parts.append(sides[j])
-                        around = functools.reduce(lambda a, b: a + b, parts)
-                        new = kb[j, base + i] * around
-                        if same is not None:
-                            new = ab[j, base + i] * same[j] + new
-                        row.append(new)
-                    nxt.append(row)
-                old = nxt
+                olds = [advance(old, step) for old in olds]
             for i in range(4):
                 r = i + (4 if side == 0 else 8)
                 for j in range(4):
-                    acc[j, r + 4] += old[i][j] * mbuf[j, pl.ds(r * mf + 8 * g, 8), :]
-        return carry
-
-    lax.fori_loop(0, steps, spread_edges, 0)
+                    total = acc[j, r + 4]
+                    for old, g in zip(olds, groups_):
+                        total = total + old[i][j] * mbuf[j, pl.ds(r * mf + 8 * g, 8), :]
+                    acc[j, r + 4] = total
+            return carry
+
+        lax.fori_loop(0, steps // together, some, 0)
+
+    pl.when(~down_end)(functools.partial(spread_edge, 0))
+    spread_edge(1)
+    pl.when(down_end)(functools.partial(spread_edge, 0))
 
     sub = lax.broadcasted_iota(jnp.int32, (12, 8, 128), 1)
     folded = []
@@ -342,33 +490,23 @@
         send(part.at[lax.rem(m + o, groups)], got.at[o - 1], o, 0) for o in (1, 2, 3)
     ]
 
-    wait_all(rim_index)
-    wait_all(rim_weight)
-    row8 = lax.broadcasted_iota(jnp.int32, (32, 128), 0)
-    lane32 = lax.broadcasted_iota(jnp.int32, (32, 128), 1)
-    in_rows = ((t > 0) | (row8 >= 8)) & ((t < tiles - 1) | (row8 < 24))
-    in_cols = jnp.where(lane32 < 64, (m < groups - 1).astype(jnp.int32), (m > 0).astype(jnp.int32))
-    in_rim = in_rows & (in_cols > 0)
+    wait_all(rim_table)
+    near = lax.broadcasted_iota(jnp.int32, (16, 128), 1) < 64
+    side_on = jnp.where(near, (m < groups - 1).astype(jnp.int32), (m > 0).astype(jnp.int32)) > 0
     for a in range(4):
-        total = jnp.zeros((32, 128), F32)
-        for s in range(4):
-            near = jnp.where(lane32 < 64, index[s, :, 256:384], index[s, :, 0:128])
-            amount = jnp.where(lane32 < 64, weight[s, :, 256:384], weight[s, :, 0:128])
-            cell = jnp.where(lane32 < 64, 4 * a, 4 * a + 3)
-            total = total + jnp.where(near == cell, amount, 0.0)
-        table_h[a] = jnp.where(in_rim, total, 0.0)
-    for b in range(4):
-        top = jnp.zeros((8, 128), F32)
-        bottom = jnp.zeros((8, 128), F32)
-        for s in range(4):
-            top = top + jnp.where(index[s, 0:8, 128:256] == 12 + b, weight[s, 0:8, 128:256], 0.0)
-            bottom = bottom + jnp.where(
-                index[s, 24:32, 128:256] == b, weight[s, 24:32, 128:256], 0.0
-            )
-        table[12 + b, 0:8] = jnp.where(t > 0, top, 0.0)
-        table[b, 24:32] = jnp.where(t < tiles - 1, bottom, 0.0)
+        both = jnp.where(near, table_col_in[1, a], table_col_in[0, a])
+        table_h[a, 8:24] = jnp.where(side_on, both, 0.0)
+    near1 = near[0:1]
+    for side, first in ((0, 12), (1, 0)):
+        on = (t > 0) if side == 0 else (t < tiles - 1)
+        row = 7 if side == 0 else 24
+        for b in range(4):
+            table[first + b, row : row + 1] = jnp.where(on, table_row_in[side, 1, b : b + 1], 0.0)
+        both = jnp.where(near1, table_row_in[side, 2, 0:1], table_row_in[side, 0, 3:4])
+        table_h[first // 4, row : row + 1] = jnp.where(side_on[0:1] & on, both, 0.0)
 
     wait_all(rim_scale)
+    unpack(scale_in, scale)
     for f in range(FIELDS):
         p = jnp.where(inside, rimmed(scale, f) * rimmed(grad, f), 0.0)
         for _ in range(STATIC_PASSES):
@@ -384,11 +522,11 @@
     for dm, dt in AROUND:
         slot = 1 - dm
         if dt == 0:
-            rims.append(send(esum.at[1], esum.at[slot], dm, dt))
+            rims.append(send_near(esum.at[1], esum.at[slot], dm, dt))
         elif dt == 1:
-            rims.append(send(esum.at[1, 72:96], eup.at[slot], dm, dt))
+            rims.append(send_near(esum.at[1, 72:96], eup.at[slot], dm, dt))
         else:
-            rims.append(send(esum.at[1, 0:24], edown.at[slot], dm, dt))
+            rims.append(send_near(esum.at[1, 0:24], edown.at[slot], dm, dt))
     wait_all(rims)
     members_all = member_count * groups
 
@@ -430,8 +568,8 @@
         for x in range(2):
             cols = slice(128 * x, 128 * x + 128)
             out_ref[f, :, cols] = 0.3 * static_buf[f, :, cols] + 2.8 * fine[x, 32 * f : 32 * f + 32]
-    for copy in sent:
-        copy.wait_send()
+    for copy, going, _ in sent:
+        only(going, copy.wait_send)
 
 
 def local(gradient, static_scale, static_rate, interp_index, interp_weight, members, spread_rate):
@@ -448,8 +586,16 @@
         scratch_shapes=[
             vmem((4, 48, 512), F32),
             vmem((4, 48, 512), F32),
-            vmem((4, 32, 384), jnp.int32),
-            vmem((4, 32, 384), F32),
+            vmem((2, 16, 256), F32),
+            vmem((2, 16, 512), F32),
+            vmem((2, 16, 256), F32),
+            vmem((2, 16, 512), F32),
+            vmem((4, 16, 128), jnp.int32),
+            vmem((4, 16, 128), F32),
+            vmem((2, 4, 16, 128), F32),
+            vmem((2, 4, 16, 128), F32),
+            vmem((2, 8, 128), F32),
+            vmem((2, 3, 8, 128), F32),
             vmem((32, 512), F32),
             vmem(members.shape, BF16),
             vmem((512, 512), BF16),
@@ -457,6 +603,7 @@
             vmem((640, 256), BF16),
             vmem((4, 16 * mf, 128), F32),
             vmem((2, 4, 4 * mf, 128), F32),
+            vmem((2, 4, mf, 128), F32),
             vmem((16, 32, 128), F32),
             vmem((4, 32, 128), F32),
             vmem((4, 192, 128), F32),

time: 60.5 us -> 43.8 us (0.72)
  the two profiles are of different devices: /device:TPU:1 before, /device:TPU:33 now
where the time goes in v2:
time: 43.8 us; the launch traced here: 43.7 us
  Pallas kernels  42.1 us (96%)
  local copies, waits for them, and re-layouts  1.57 us (4%)
    pallas_call x1, Pallas kernels, local(): pl.pallas_call(kernel, out_shape=jax.ShapeDtypeStruct(gradient.shape, F32...  42.1 us
    unnamed x1, local copies, waits for them, and re-layouts  1.57 us

profile of v2, /device:TPU:33, one launch (start us, length us, event | category | flops | bytes accessed | tf_op | source)
XLA Modules:
  0.0 43.7 jit_solution(16653442730315816239)
XLA Ops:
  0.0 42.1 %shard_map.73 = f32[4,32,256]{2,1,0:T(8,128)} custom-call(f32[4]{0:T(128)} %rate_ref.1, f32[4,32,256]{2,1,0:T(8,128)} %grad_hbm.1, f32[4,32,256]{2,1,0:T(8,128)} %scale_hbm.1, s32[4,16,128]{2,1,0:T(8,128)} %index_hbm.1, f32[4,16,128]{2,1,0:T(8,128)} %weight_hbm.1, bf16[20,4,16,512]{3,2,1,0:T(8,128)(2,1)} %members_hbm.1, f32[16,512]{1,0:T(8,128)} %spread_hbm.1), custom_call_target="tpu_custom_call" | custom-call | tf_op jit(solution)/shard_map/pallas_call | solution.py:581
  42.1 1.6 %copy.9 = f32[4,32,256]{2,1,0:T(8,128)} copy(f32[4,32,256]{2,1,0:T(8,128)} %shard_map.73) | data formatting | bytes 262144

commit v3 on v2

--- a/solution.py
+++ b/solution.py
@@ -15,7 +15,7 @@
 F32 = jnp.float32
 BF16 = jnp.bfloat16
 AROUND = [(0, 1), (0, -1), (1, 0), (-1, 0), (1, 1), (1, -1), (-1, 1), (-1, -1)]
-CHUNK = 4
+CHUNK = 1
 ZROW = 16
 
 
@@ -48,12 +48,12 @@
 
 
 def kernel(
-    rate_ref, grad_hbm, scale_hbm, index_hbm, weight_hbm, members_hbm, spread_hbm, out_ref,
+    rate_hbm, grad_hbm, scale_hbm, index_hbm, weight_hbm, members_hbm, spread_hbm, static_ref, fine_ref,
     grad, scale, grad_out, grad_in, scale_out, scale_in, index, weight,
     table_col, table_col_in, table_row, table_row_in, spread, raw, perm, pick, place,
     mbuf, edge, passing, table, table_h, picked, coarse, coarse_e, cperm, cb, ceb, kb, ab,
-    pa, pb, acc, halo_v, part, got, esum, eup, edown, eall, lhs, fine, static_buf,
-    local_sem, send_sem, recv_sem,
+    pa, pb, acc, halo_v, part, got, esum, eup, edown, eall, lhs, fine,
+    rate_ref, local_sem, send_sem, recv_sem,
 ):
     m, t = lax.axis_index("mem"), lax.axis_index("tile")
     groups, tiles = lax.axis_size("mem"), lax.axis_size("tile")
@@ -116,6 +116,7 @@
     fetch_index = fetch(index_hbm, index)
     fetch_weight = fetch(weight_hbm, weight)
     fetch_spread = fetch(spread_hbm, spread.at[8:24])
+    fetch_rate = fetch(rate_hbm, rate_ref)
     fetch_scale = fetch(scale_hbm, scale.at[:, 8:40, 128:384])
 
     sent = []
@@ -505,6 +506,7 @@
         both = jnp.where(near1, table_row_in[side, 2, 0:1], table_row_in[side, 0, 3:4])
         table_h[first // 4, row : row + 1] = jnp.where(side_on[0:1] & on, both, 0.0)
 
+    fetch_rate.wait()
     wait_all(rim_scale)
     unpack(scale_in, scale)
     for f in range(FIELDS):
@@ -514,7 +516,7 @@
                 pltpu.roll(p, 1, 1) + pltpu.roll(p, 383, 1)
             )
             p = jnp.where(inside, p + rate_ref[f] * (around - 4.0 * p), 0.0)
-        static_buf[f] = scale[f, 8:40, 128:384] * p[8:40, 0:256]
+        static_ref[f] = scale[f, 8:40, 128:384] * p[8:40, 0:256]
 
     wait_all(shares)
     esum[1] = (part[m] + got[0]) + (got[1] + got[2])
@@ -567,7 +569,7 @@
     for f in range(FIELDS):
         for x in range(2):
             cols = slice(128 * x, 128 * x + 128)
-            out_ref[f, :, cols] = 0.3 * static_buf[f, :, cols] + 2.8 * fine[x, 32 * f : 32 * f + 32]
+            fine_ref[f, :, cols] = fine[x, 32 * f : 32 * f + 32]
     for copy, going, _ in sent:
         only(going, copy.wait_send)
 
@@ -578,11 +580,11 @@
     anywhere = pl.BlockSpec(memory_space=pl.ANY)
     vmem = pltpu.VMEM
     sems = 64
-    return pl.pallas_call(
+    static, fine = pl.pallas_call(
         kernel,
-        out_shape=jax.ShapeDtypeStruct(gradient.shape, F32),
-        in_specs=[pl.BlockSpec(memory_space=pltpu.SMEM)] + [anywhere] * 6,
-        out_specs=pl.BlockSpec(memory_space=pltpu.VMEM),
+        out_shape=[jax.ShapeDtypeStruct(gradient.shape, F32)] * 2,
+        in_specs=[anywhere] * 7,
+        out_specs=[pl.BlockSpec(memory_space=pltpu.VMEM)] * 2,
         scratch_shapes=[
             vmem((4, 48, 512), F32),
             vmem((4, 48, 512), F32),
@@ -626,15 +628,16 @@
             vmem((3, 96, 128), F32),
             vmem((128, 640), F32),
             vmem((2, 128, 128), F32),
-            vmem((4, 32, 256), F32),
-            pltpu.SemaphoreType.DMA((6,)),
+            pltpu.SMEM((4,), F32),
+            pltpu.SemaphoreType.DMA((7,)),
             pltpu.SemaphoreType.DMA((sems,)),
             pltpu.SemaphoreType.DMA((sems,)),
         ],
         compiler_params=pltpu.CompilerParams(
-            collective_id=0, has_side_effects=True, vmem_limit_bytes=56 << 20
+            collective_id=0, has_side_effects=True, vmem_limit_bytes=18 << 20
         ),
-    )(static_rate, gradient, static_scale, interp_index, interp_weight, members, spread_rate)
+    )(*[pltpu.with_memory_space_constraint(x, pltpu.HBM) for x in (static_rate, gradient, static_scale, interp_index, interp_weight, members, spread_rate)])
+    return 0.3 * static + 2.8 * fine
 
 
 def solution(mesh):

time: 43.8 us -> 41.3 us (0.943)
  Pallas kernels: 42.1 us -> 40.5 us
  local copies, waits for them, and re-layouts: 1.57 us -> 0 us
  other arithmetic: 0 us -> 0.68 us
    pallas_call x1, Pallas kernels: 42.1 us -> 40.5 us  [local(): pl.pallas_call(kernel, out_shape=[jax.ShapeDtypeStruct(gradient.shape, F3...]
    unnamed x1 -> x0, local copies, waits for them, and re-layouts: 1.57 us -> none
    add x0 -> x1, other arithmetic: none -> 0.68 us  [local(): return 0.3 * static + 2.8 * fine]
where the time goes in v3:
time: 41.3 us; the launch traced here: 41.2 us
  Pallas kernels  40.5 us (98%)
  other arithmetic  0.68 us (2%)
    pallas_call x1, Pallas kernels, local(): pl.pallas_call(kernel, out_shape=[jax.ShapeDtypeStruct(gradient.shape, F3...  40.5 us

profile of v3, /device:TPU:33, one launch (start us, length us, event | category | flops | bytes accessed | tf_op | source)
XLA Modules:
  0.0 41.2 jit_solution(8624153215248366289)
XLA Ops:
  0.0 40.5 %shard_map.73 = (f32[4,32,256]{2,1,0:T(8,128)S(1)}, f32[4,32,256]{2,1,0:T(8,128)S(1)}) custom-call(f32[4]{0:T(128)} %rate_hbm.1, f32[4,32,256]{2,1,0:T(8,128)} %grad_hbm.1, f32[4,32,256]{2,1,0:T(8,128)} %scale_hbm.1, s32[4,16,128]{2,1,0:T(8,128)} %index_hbm.1, f32[4,16,128]{2,1,0:T(8,128)} %weight_hbm.1, bf16[20,4,16,512]{3,2,1,0:T(8,128)(2,1)} %members_hbm.1, ...), custom_call_target="tpu_custom_call" | custom-call | tf_op jit(solution)/shard_map/pallas_call | solution.py:583
  40.5 0.7 %multiply_add_fusion = f32[4,32,256]{2,1,0:T(8,128)} fusion(f32[4,32,256]{2,1,0:T(8,128)S(1)} %get-tuple-element.8, f32[4,32,256]{2,1,0:T(8,128)S(1)} %get-tuple-element.7), kind=kLoop, calls=%fused_computation | loop fusion | flops 98304 | bytes 393216 | tf_op jit(solution)/shard_map/add | solution.py:640

commit v4 on v3

--- a/solution.py
+++ b/solution.py
@@ -15,7 +15,6 @@
 F32 = jnp.float32
 BF16 = jnp.bfloat16
 AROUND = [(0, 1), (0, -1), (1, 0), (-1, 0), (1, 1), (1, -1), (-1, 1), (-1, -1)]
-CHUNK = 1
 ZROW = 16
 
 
@@ -35,10 +34,6 @@
     return max(-step, step - SPREAD_PASSES - REACH)
 
 
-def row_chunks(low, high):
-    return [(r, min(r + CHUNK - 1, high)) for r in range(low, high + 1, CHUNK)]
-
-
 def beside(row, lane):
     axis = row[0].ndim - 1
     zero = jnp.zeros_like(row[0])
@@ -51,7 +46,7 @@
     rate_hbm, grad_hbm, scale_hbm, index_hbm, weight_hbm, members_hbm, spread_hbm, static_ref, fine_ref,
     grad, scale, grad_out, grad_in, scale_out, scale_in, index, weight,
     table_col, table_col_in, table_row, table_row_in, spread, raw, perm, pick, place,
-    mbuf, edge, passing, table, table_h, picked, coarse, coarse_e, cperm, cb, ceb, kb, ab,
+    mbuf, edge, passing, table, table_h, picked, coarse, coarse_out, coarse_e, cperm, cb, ceb, kb, ab,
     pa, pb, acc, halo_v, part, got, esum, eup, edown, eall, lhs, fine,
     rate_ref, local_sem, send_sem, recv_sem,
 ):
@@ -168,16 +163,6 @@
     target = lax.broadcasted_iota(jnp.int32, (512, 512), 1)
     perm[...] = (source == 4 * (target & 127) + (target >> 7)).astype(F32).astype(BF16)
 
-    fetch_grad.wait()
-    pack(grad, grad_out)
-    fetch_spread.wait()
-    pl.semaphore_wait(barrier, waited)
-    rim_grad = send_rim(grad, grad_out, grad_in)
-    rim_spread = [
-        send_near(spread.at[16:24], spread.at[0:8], 0, 1),
-        send_near(spread.at[8:16], spread.at[24:32], 0, -1),
-    ]
-
     fetch_members.wait()
 
     half = member_count // 2
@@ -196,6 +181,16 @@
 
     convert(0)
     convert(1)
+    fetch_grad.wait()
+    pack(grad, grad_out)
+    fetch_spread.wait()
+    pl.semaphore_wait(barrier, waited)
+    rim_grad = send_rim(grad, grad_out, grad_in)
+    rim_spread = [
+        send_near(spread.at[16:24], spread.at[0:8], 0, 1),
+        send_near(spread.at[8:16], spread.at[24:32], 0, -1),
+    ]
+
     edge_members, late = [[], []], []
     for rows in (range(0, 1), range(1, 2), range(2, 4)):
         first, count = rows[0] * mf, len(rows) * mf
@@ -322,9 +317,13 @@
 
     wait_all(all_coarse)
     pass_on(0)
+    for q in range(4):
+        for f in range(FIELDS):
+            coarse_out[0, q, 4 * f : 4 * f + 4] = coarse[q, f, 0:4]
+            coarse_out[1, q, 4 * f : 4 * f + 4] = coarse[q, f, 12:16]
     edge_coarse = [
-        send_near(coarse.at[:, :, 8:16], coarse_e.at[0], 0, 1),
-        send_near(coarse.at[:, :, 0:8], coarse_e.at[1], 0, -1),
+        send_near(coarse_out.at[1], coarse_e.at[0], 0, 1),
+        send_near(coarse_out.at[0], coarse_e.at[1], 0, -1),
     ]
     rim_scale = send_rim(scale, scale_out, scale_in)
     rim_table = []
@@ -348,75 +347,78 @@
             cb[j, r, 0:4] = four
             cb[j, r, 4:8] = four
 
-    zero2 = jnp.zeros((2, 8, 128), F32)
-
-    def spread_own(g, carry):
-        @pl.when(g == steps // 2)
+    lane8 = lax.broadcasted_iota(jnp.int32, (8, 128), 1)
+    together = 2 if steps % 2 == 0 else 1
+
+    def spread_own(i, carry):
+        @pl.when(i == steps // together // 2)
         def _():
             pass_on(1)
 
-        bufs = [pa, pb]
-        for j in range(4):
-            for r in range(16):
-                pa[j, r + 8] = mbuf[j, pl.ds(r * mf + 8 * g, 8), :] * cb[j, r]
-            pa[j, 6:8] = zero2
-            pa[j, 24:26] = zero2
+        taken = [together * i + k for k in range(together)]
+        for r in range(16):
+            for j in range(4):
+                c = cb[j, r]
+                for k, g in enumerate(taken):
+                    pa[k, j, r + 8] = mbuf[j, pl.ds(r * mf + 8 * g, 8), :] * c
+        filled = (0, 15)
         for step in range(1, SPREAD_PASSES + 1):
-            src, dst = bufs[(step - 1) % 2], bufs[step % 2]
+            src, dst = (pa, pb) if step % 2 else (pb, pa)
+
+            def line(k, r):
+                if not filled[0] <= r <= filled[1]:
+                    return None
+                return [src[k, j, r + 8] for j in range(4)]
+
             low = first_row(step)
             high = 15 - low
-            if step <= 6:
-                for j in range(4):
-                    dst[j, low + 6 : low + 8] = zero2
-                    dst[j, high + 9 : high + 11] = zero2
-            last = step == SPREAD_PASSES
-            if last:
-                pieces = row_chunks(-REACH, -1) + row_chunks(0, 15) + row_chunks(16, 15 + REACH)
-            else:
-                pieces = row_chunks(low, high)
-            for r0, r1 in pieces:
-                n = r1 - r0 + 1
-                lane = lax.broadcasted_iota(jnp.int32, (n, 8, 128), 2)
-                x = [src[j, r0 + 7 : r1 + 10] for j in range(4)]
-                centre = [v[1 : n + 1] for v in x]
-                sides = beside(centre, lane)
-                for j in range(4):
-                    around = (x[j][0:n] + x[j][2 : n + 2]) + sides[j]
-                    new = ab[j, r0 + 8 : r1 + 9] * centre[j] + kb[j, r0 + 8 : r1 + 9] * around
-                    if not last:
-                        dst[j, r0 + 8 : r1 + 9] = new
-                    elif r0 < 0:
-                        halo_v[g, j, r0 + 4 : r1 + 5] = new
-                    elif r0 >= 16:
-                        halo_v[g, j, r0 - 12 : r1 - 11] = new
-                    else:
-                        for r in range(r0, r1 + 1):
-                            acc[j, r + 4] += new[r - r0] * mbuf[j, pl.ds(r * mf + 8 * g, 8), :]
+            above = [line(k, low - 1) for k in range(together)]
+            here = [line(k, low) for k in range(together)]
+            for r in range(low, high + 1):
+                below = [line(k, r + 1) for k in range(together)]
+                rate_r = [kb[j, r + 8] for j in range(4)]
+                stay_r = [ab[j, r + 8] for j in range(4)] if here[0] is not None else None
+                for k, g in enumerate(taken):
+                    sides = beside(here[k], lane8) if stay_r is not None else None
+                    for j in range(4):
+                        parts = [row[k][j] for row in (above, below) if row[k] is not None]
+                        if sides is not None:
+                            parts.append(sides[j])
+                        new = rate_r[j] * functools.reduce(lambda a, b: a + b, parts)
+                        if stay_r is not None:
+                            new = stay_r[j] * here[k][j] + new
+                        if step < SPREAD_PASSES:
+                            dst[k, j, r + 8] = new
+                        elif r < 0:
+                            halo_v[g, j, r + 4] = new
+                        elif r >= 16:
+                            halo_v[g, j, r - 12] = new
+                        else:
+                            acc[j, r + 4] += new * mbuf[j, pl.ds(r * mf + 8 * g, 8), :]
+                above, here = here, below
+            filled = (low, high)
         return carry
 
-    lax.fori_loop(0, steps, spread_own, 0)
+    lax.fori_loop(0, steps // together, spread_own, 0)
 
     wait_all(edge_coarse)
     rows = jnp.concatenate(
         [
-            jnp.concatenate([coarse_e[side, q].reshape(32, 128) for q in range(4)], axis=1)
+            jnp.concatenate([coarse_e[side, q] for q in range(4)], axis=1)
             for side in range(2)
         ],
         axis=0,
     )
     out = split_dot(rows, perm[...])
     for j in range(4):
-        cperm[j, 0:64] = out[:, 128 * j : 128 * j + 128]
+        cperm[j, 0:32] = out[:, 128 * j : 128 * j + 128]
     for side in range(2):
         known = (t > 0) if side == 0 else (t < tiles - 1)
         for j in range(4):
             for r in range(4):
-                start = 32 * side + (4 + r if side == 0 else r)
-                four = jnp.where(known, cperm[j, pl.ds(start, 4, stride=8), :], 0.0)
+                four = jnp.where(known, cperm[j, pl.ds(16 * side + r, 4, stride=4), :], 0.0)
                 ceb[side, j, r, 0:4] = four
                 ceb[side, j, r, 4:8] = four
-    lane8 = lax.broadcasted_iota(jnp.int32, (8, 128), 1)
-
     def spread_edge(side):
         wait_all(edge_members[side])
         only(down_end & feeder if side == 0 else up_end & feeder, onward[0][0].wait_recv)
@@ -442,8 +444,6 @@
                     row.append(new)
                 nxt.append(row)
             return nxt
-
-        together = 2 if steps % 2 == 0 else 1
 
         def some(i, carry):
             groups_ = [together * i + k for k in range(together)]
@@ -474,22 +474,38 @@
 
         lax.fori_loop(0, steps // together, some, 0)
 
-    pl.when(~down_end)(functools.partial(spread_edge, 0))
-    spread_edge(1)
-    pl.when(down_end)(functools.partial(spread_edge, 0))
-
-    sub = lax.broadcasted_iota(jnp.int32, (12, 8, 128), 1)
-    folded = []
-    for j in range(4):
-        x = acc[j]
-        y = (x + pltpu.roll(x, 4, 1)).reshape(12, 2, 8, 128)
-        folded.append(jnp.where(sub < 4, y[:, 0], y[:, 1]).reshape(96, 128))
-    out = split_dot(jnp.concatenate(folded, axis=1), perm[...], transposed=True)
-    for q in range(4):
-        part[q] = out[:, 128 * q : 128 * q + 128]
     shares = [
-        send(part.at[lax.rem(m + o, groups)], got.at[o - 1], o, 0) for o in (1, 2, 3)
+        [
+            send(
+                part.at[lax.rem(m + o, groups), 48 * side : 48 * side + 48],
+                got.at[o - 1, 48 * side : 48 * side + 48],
+                o, 0, start=False,
+            )
+            for o in (1, 2, 3)
+        ]
+        for side in range(2)
     ]
+    sub = lax.broadcasted_iota(jnp.int32, (6, 8, 128), 1)
+
+    def share(side):
+        folded = []
+        for j in range(4):
+            x = acc[j, 12 * side : 12 * side + 12]
+            y = (x + pltpu.roll(x, 4, 1)).reshape(6, 2, 8, 128)
+            folded.append(jnp.where(sub < 4, y[:, 0], y[:, 1]).reshape(48, 128))
+        out = split_dot(jnp.concatenate(folded, axis=1), perm[...], transposed=True)
+        for q in range(4):
+            part[q, 48 * side : 48 * side + 48] = out[:, 128 * q : 128 * q + 128]
+        for copy, _, _ in shares[side]:
+            copy.start()
+
+    def finish(side):
+        only(there(0, 1 if side else -1), functools.partial(spread_edge, side))
+        share(side)
+
+    pl.when(~down_end)(functools.partial(finish, 0))
+    finish(1)
+    pl.when(down_end)(functools.partial(finish, 0))
 
     wait_all(rim_table)
     near = lax.broadcasted_iota(jnp.int32, (16, 128), 1) < 64
@@ -518,7 +534,7 @@
             p = jnp.where(inside, p + rate_ref[f] * (around - 4.0 * p), 0.0)
         static_ref[f] = scale[f, 8:40, 128:384] * p[8:40, 0:256]
 
-    wait_all(shares)
+    wait_all(shares[0] + shares[1])
     esum[1] = (part[m] + got[0]) + (got[1] + got[2])
     rims = []
     for dm, dt in AROUND:
@@ -610,14 +626,15 @@
             vmem((4, 32, 128), F32),
             vmem((4, 192, 128), F32),
             vmem((4, 4, 16, 128), F32),
-            vmem((2, 4, 4, 8, 128), F32),
+            vmem((2, 4, 16, 128), F32),
+            vmem((2, 4, 16, 128), F32),
             vmem((4, 64, 128), F32),
             vmem((4, 16, 8, 128), F32),
             vmem((2, 4, 4, 8, 128), F32),
             vmem((4, 32, 8, 128), F32),
             vmem((4, 32, 8, 128), F32),
-            vmem((4, 32, 8, 128), F32),
-            vmem((4, 32, 8, 128), F32),
+            vmem((2, 4, 32, 8, 128), F32),
+            vmem((2, 4, 32, 8, 128), F32),
             vmem((4, 24, 8, 128), F32),
             vmem((mf // 8, 4, 8, 8, 128), F32),
             vmem((4, 96, 128), F32),

time: 41.3 us -> 39.1 us (0.947)
  Pallas kernels: 40.5 us -> 38.3 us
    pallas_call x1, Pallas kernels: 40.5 us -> 38.3 us  [local(): pl.pallas_call(kernel, out_shape=[jax.ShapeDtypeStruct(gradient.shape, F3...]
where the time goes in v4:
time: 39.1 us; the launch traced here: 39 us
  Pallas kernels  38.3 us (98%)
  other arithmetic  0.68 us (2%)
    pallas_call x1, Pallas kernels, local(): pl.pallas_call(kernel, out_shape=[jax.ShapeDtypeStruct(gradient.shape, F3...  38.3 us

profile of v4, /device:TPU:33, one launch (start us, length us, event | category | flops | bytes accessed | tf_op | source)
XLA Modules:
  0.0 39.0 jit_solution(10054440875608633634)
XLA Ops:
  0.0 38.3 %shard_map.73 = (f32[4,32,256]{2,1,0:T(8,128)S(1)}, f32[4,32,256]{2,1,0:T(8,128)S(1)}) custom-call(f32[4]{0:T(128)} %rate_hbm.1, f32[4,32,256]{2,1,0:T(8,128)} %grad_hbm.1, f32[4,32,256]{2,1,0:T(8,128)} %scale_hbm.1, s32[4,16,128]{2,1,0:T(8,128)} %index_hbm.1, f32[4,16,128]{2,1,0:T(8,128)} %weight_hbm.1, bf16[20,4,16,512]{3,2,1,0:T(8,128)(2,1)} %members_hbm.1, ...), custom_call_target="tpu_custom_call" | custom-call | tf_op jit(solution)/shard_map/pallas_call | solution.py:599
  38.3 0.7 %multiply_add_fusion = f32[4,32,256]{2,1,0:T(8,128)} fusion(f32[4,32,256]{2,1,0:T(8,128)S(1)} %get-tuple-element.8, f32[4,32,256]{2,1,0:T(8,128)S(1)} %get-tuple-element.7), kind=kLoop, calls=%fused_computation | loop fusion | flops 98304 | bytes 393216 | tf_op jit(solution)/shard_map/add | solution.py:657

commit v5 on v4

--- a/solution.py
+++ b/solution.py
@@ -47,7 +47,7 @@
     grad, scale, grad_out, grad_in, scale_out, scale_in, index, weight,
     table_col, table_col_in, table_row, table_row_in, spread, raw, perm, pick, place,
     mbuf, edge, passing, table, table_h, picked, coarse, coarse_out, coarse_e, cperm, cb, ceb, kb, ab,
-    pa, pb, acc, halo_v, part, got, esum, eup, edown, eall, lhs, fine,
+    pa, pb, acc, halo_v, part, part_x, got, got_x, esum, eup, edown, eall, lhs, fine,
     rate_ref, local_sem, send_sem, recv_sem,
 ):
     m, t = lax.axis_index("mem"), lax.axis_index("tile")
@@ -209,19 +209,20 @@
                 late.append((going & cross, entry[0]))
     origin = jnp.where(up_end, 12 * mf, 0)
     over_z, onward = [], []
-    for row in range(2):
-        from_row = pl.ds(pl.multiple_of(origin + row * mf, mf), mf)
+    middle = mf + mf // 16 * 8
+    for low, high in ((0, mf), (mf, middle), (middle, 2 * mf)):
+        from_row = pl.ds(pl.multiple_of(origin + low, 8), high - low)
+        rows = pl.ds(low, high - low)
         over_z.append(
-            send(mbuf.at[:, from_row], passing.at[row], 0, over, feeder, relay, start=row == 0)
+            send(mbuf.at[:, from_row], passing.at[:, rows], 0, over, feeder, relay, start=low == 0)
         )
         onward.append(
             send(
-                passing.at[row],
-                edge.at[down_end.astype(jnp.int32), :, pl.ds(row * mf, mf)],
+                passing.at[:, rows], edge.at[down_end.astype(jnp.int32), :, rows],
                 0, along, relay, feeder, start=False,
             )
         )
-    late.append((feeder, over_z[1][0]))
+    late += [(feeder, copy) for copy, _, _ in over_z[1:]]
 
     fetch_index.wait()
     fetch_weight.wait()
@@ -351,9 +352,10 @@
     together = 2 if steps % 2 == 0 else 1
 
     def spread_own(i, carry):
-        @pl.when(i == steps // together // 2)
-        def _():
-            pass_on(1)
+        for piece, when in ((1, 1), (2, 3)):
+            @pl.when(i == min(when, steps // together - 1))
+            def _():
+                pass_on(piece)
 
         taken = [together * i + k for k in range(together)]
         for r in range(16):
@@ -419,11 +421,20 @@
                 four = jnp.where(known, cperm[j, pl.ds(16 * side + r, 4, stride=4), :], 0.0)
                 ceb[side, j, r, 0:4] = four
                 ceb[side, j, r, 4:8] = four
+    def meet_edge(side):
+        wait_all(edge_members[side])
+        for copy, _, _ in onward:
+            only(down_end & feeder if side == 0 else up_end & feeder, copy.wait_recv)
+
+        for r in range(4):
+            for j in range(4):
+                terms = [
+                    edge[side, j, pl.ds(r * mf + 8 * g, 8), :] * halo_v[g, j, 4 * side + r]
+                    for g in range(steps)
+                ]
+                acc[j, r if side == 0 else 20 + r] = functools.reduce(lambda a, b: a + b, terms)
+
     def spread_edge(side):
-        wait_all(edge_members[side])
-        only(down_end & feeder if side == 0 else up_end & feeder, onward[0][0].wait_recv)
-        only(down_end & feeder if side == 0 else up_end & feeder, onward[1][0].wait_recv)
-
         def advance(old, step):
             base = 8 + (step - REACH if side == 0 else 16 - step)
             shift = 1 if side == 0 else -1
@@ -450,13 +461,9 @@
             fields = []
             for r in range(4):
                 for j in range(4):
-                    to = r if side == 0 else 20 + r
-                    total = acc[j, to]
-                    for k, g in enumerate(groups_):
+                    for g in groups_:
                         theirs = edge[side, j, pl.ds(r * mf + 8 * g, 8), :]
-                        total = total + theirs * halo_v[g, j, 4 * side + r]
                         fields.append(theirs * ceb[side, j, r])
-                    acc[j, to] = total
             olds = [
                 [[fields[(4 * r + j) * together + k] for j in range(4)] for r in range(4)]
                 for k in range(together)
@@ -474,38 +481,51 @@
 
         lax.fori_loop(0, steps // together, some, 0)
 
-    shares = [
-        [
-            send(
-                part.at[lax.rem(m + o, groups), 48 * side : 48 * side + 48],
-                got.at[o - 1, 48 * side : 48 * side + 48],
-                o, 0, start=False,
-            )
-            for o in (1, 2, 3)
-        ]
-        for side in range(2)
+    spans = [(0, 32), (64, 96), (32, 64)]
+    shares = []
+    for low, high in spans:
+        shares.append(
+            [
+                send(
+                    part.at[lax.rem(m + o, groups), low:high], got.at[o - 1, low:high], o, 0,
+                    start=False,
+                )
+                for o in (1, 2, 3)
+            ]
+        )
+    shares[2] += [
+        send(part_x.at[lax.rem(m + o, groups)], got_x.at[o - 1], o, 0, start=False)
+        for o in (1, 2, 3)
     ]
-    sub = lax.broadcasted_iota(jnp.int32, (6, 8, 128), 1)
-
-    def share(side):
+    sub = lax.broadcasted_iota(jnp.int32, (4, 8, 128), 1)
+    near32 = lax.broadcasted_iota(jnp.int32, (32, 128), 1) < 64
+
+    def share(piece):
+        low, high = spans[piece]
         folded = []
         for j in range(4):
-            x = acc[j, 12 * side : 12 * side + 12]
-            y = (x + pltpu.roll(x, 4, 1)).reshape(6, 2, 8, 128)
-            folded.append(jnp.where(sub < 4, y[:, 0], y[:, 1]).reshape(48, 128))
+            x = acc[j, low // 4 : high // 4]
+            y = (x + pltpu.roll(x, 4, 1)).reshape(4, 2, 8, 128)
+            folded.append(jnp.where(sub < 4, y[:, 0], y[:, 1]).reshape(32, 128))
         out = split_dot(jnp.concatenate(folded, axis=1), perm[...], transposed=True)
+        quarters = [out[:, 128 * q : 128 * q + 128] for q in range(4)]
         for q in range(4):
-            part[q, 48 * side : 48 * side + 48] = out[:, 128 * q : 128 * q + 128]
-        for copy, _, _ in shares[side]:
+            part[q, low:high] = quarters[q]
+            if piece == 2:
+                part_x[q] = jnp.where(near32, quarters[min(q + 1, 3)], quarters[max(q - 1, 0)])
+        for copy, _, _ in shares[piece]:
             copy.start()
 
     def finish(side):
-        only(there(0, 1 if side else -1), functools.partial(spread_edge, side))
+        exists = there(0, 1 if side else -1)
+        only(exists, functools.partial(meet_edge, side))
         share(side)
+        only(exists, functools.partial(spread_edge, side))
 
     pl.when(~down_end)(functools.partial(finish, 0))
     finish(1)
     pl.when(down_end)(functools.partial(finish, 0))
+    share(2)
 
     wait_all(rim_table)
     near = lax.broadcasted_iota(jnp.int32, (16, 128), 1) < 64
@@ -522,6 +542,22 @@
         both = jnp.where(near1, table_row_in[side, 2, 0:1], table_row_in[side, 0, 3:4])
         table_h[first // 4, row : row + 1] = jnp.where(side_on[0:1] & on, both, 0.0)
 
+    rims = []
+    for piece, (low, high) in enumerate(spans[:2]):
+        wait_all(shares[piece])
+        esum[1, low:high] = (part[m, low:high] + got[0, low:high]) + (
+            got[1, low:high] + got[2, low:high]
+        )
+    for dm, dt in AROUND:
+        slot = 1 - dm
+        if dt == 0:
+            for low, high in spans[:2]:
+                rims.append(send_near(esum.at[1, low:high], esum.at[slot, low:high], dm, dt))
+        elif dt == 1:
+            rims.append(send_near(esum.at[1, 72:96], eup.at[slot], dm, dt))
+        else:
+            rims.append(send_near(esum.at[1, 0:24], edown.at[slot], dm, dt))
+
     fetch_rate.wait()
     wait_all(rim_scale)
     unpack(scale_in, scale)
@@ -534,22 +570,14 @@
             p = jnp.where(inside, p + rate_ref[f] * (around - 4.0 * p), 0.0)
         static_ref[f] = scale[f, 8:40, 128:384] * p[8:40, 0:256]
 
-    wait_all(shares[0] + shares[1])
-    esum[1] = (part[m] + got[0]) + (got[1] + got[2])
-    rims = []
-    for dm, dt in AROUND:
-        slot = 1 - dm
-        if dt == 0:
-            rims.append(send_near(esum.at[1], esum.at[slot], dm, dt))
-        elif dt == 1:
-            rims.append(send_near(esum.at[1, 72:96], eup.at[slot], dm, dt))
-        else:
-            rims.append(send_near(esum.at[1, 0:24], edown.at[slot], dm, dt))
+    wait_all(shares[2])
+    esum[1, 32:64] = (part[m, 32:64] + got[0, 32:64]) + (got[1, 32:64] + got[2, 32:64])
     wait_all(rims)
     members_all = member_count * groups
 
     def whole(slot):
-        eall[slot] = esum[slot]
+        for low, high in spans if slot == 1 else spans[:2]:
+            eall[slot, low:high] = esum[slot, low:high]
         eall[slot, 8:32] += eup[slot]
         eall[slot, 64:88] += edown[slot]
 
@@ -559,6 +587,7 @@
     side_e = jnp.where(lane96 < 64, eall[2], eall[0]) / (members_all - 1)
     eall[1] = eall[1] / (members_all - 1)
     eall[0] = side_e
+    eall[0, 32:64] = ((part_x[m] + got_x[0]) + (got_x[1] + got_x[2])) / (members_all - 1)
     for parity in range(2):
         pairs = [(1, 0), (3, -1)] if parity == 0 else [(2, 0), (0, 1)]
         for f in range(FIELDS):
@@ -595,7 +624,7 @@
     mf = member_count * FIELDS
     anywhere = pl.BlockSpec(memory_space=pl.ANY)
     vmem = pltpu.VMEM
-    sems = 64
+    sems = 80
     static, fine = pl.pallas_call(
         kernel,
         out_shape=[jax.ShapeDtypeStruct(gradient.shape, F32)] * 2,
@@ -621,7 +650,7 @@
             vmem((640, 256), BF16),
             vmem((4, 16 * mf, 128), F32),
             vmem((2, 4, 4 * mf, 128), F32),
-            vmem((2, 4, mf, 128), F32),
+            vmem((4, 2 * mf, 128), F32),
             vmem((16, 32, 128), F32),
             vmem((4, 32, 128), F32),
             vmem((4, 192, 128), F32),
@@ -638,7 +667,9 @@
             vmem((4, 24, 8, 128), F32),
             vmem((mf // 8, 4, 8, 8, 128), F32),
             vmem((4, 96, 128), F32),
+            vmem((4, 32, 128), F32),
             vmem((3, 96, 128), F32),
+            vmem((3, 32, 128), F32),
             vmem((3, 96, 128), F32),
             vmem((3, 24, 128), F32),
             vmem((3, 24, 128), F32),

time: 39.1 us -> 38.3 us (0.980)
  Pallas kernels: 38.3 us -> 37.5 us
    pallas_call x1, Pallas kernels: 38.3 us -> 37.5 us  [local(): pl.pallas_call(kernel, out_shape=[jax.ShapeDtypeStruct(gradient.shape, F3...]
where the time goes in v5:
time: 38.3 us; the launch traced here: 38.2 us
  Pallas kernels  37.5 us (98%)
  other arithmetic  0.68 us (2%)
    pallas_call x1, Pallas kernels, local(): pl.pallas_call(kernel, out_shape=[jax.ShapeDtypeStruct(gradient.shape, F3...  37.5 us

profile of v5, /device:TPU:33, one launch (start us, length us, event | category | flops | bytes accessed | tf_op | source)
XLA Modules:
  0.0 38.2 jit_solution(4443542204321752722)
XLA Ops:
  0.0 37.5 %shard_map.73 = (f32[4,32,256]{2,1,0:T(8,128)S(1)}, f32[4,32,256]{2,1,0:T(8,128)S(1)}) custom-call(f32[4]{0:T(128)} %rate_hbm.1, f32[4,32,256]{2,1,0:T(8,128)} %grad_hbm.1, f32[4,32,256]{2,1,0:T(8,128)} %scale_hbm.1, s32[4,16,128]{2,1,0:T(8,128)} %index_hbm.1, f32[4,16,128]{2,1,0:T(8,128)} %weight_hbm.1, bf16[20,4,16,512]{3,2,1,0:T(8,128)(2,1)} %members_hbm.1, ...), custom_call_target="tpu_custom_call" | custom-call | tf_op jit(solution)/shard_map/pallas_call | solution.py:628
  37.5 0.7 %multiply_add_fusion = f32[4,32,256]{2,1,0:T(8,128)} fusion(f32[4,32,256]{2,1,0:T(8,128)S(1)} %get-tuple-element.8, f32[4,32,256]{2,1,0:T(8,128)S(1)} %get-tuple-element.7), kind=kLoop, calls=%fused_computation | loop fusion | flops 98304 | bytes 393216 | tf_op jit(solution)/shard_map/add | solution.py:688

commit v6 on v5

--- a/solution.py
+++ b/solution.py
@@ -45,7 +45,7 @@
 def kernel(
     rate_hbm, grad_hbm, scale_hbm, index_hbm, weight_hbm, members_hbm, spread_hbm, static_ref, fine_ref,
     grad, scale, grad_out, grad_in, scale_out, scale_in, index, weight,
-    table_col, table_col_in, table_row, table_row_in, spread, raw, perm, pick, place,
+    table_col, table_col_in, spread, raw, perm, pick, place,
     mbuf, edge, passing, table, table_h, picked, coarse, coarse_out, coarse_e, cperm, cb, ceb, kb, ab,
     pa, pb, acc, halo_v, part, part_x, got, got_x, esum, eup, edown, eall, lhs, fine,
     rate_ref, local_sem, send_sem, recv_sem,
@@ -192,12 +192,12 @@
     ]
 
     edge_members, late = [[], []], []
-    for rows in (range(0, 1), range(1, 2), range(2, 4)):
+    for rows in (range(0, 2), range(2, 4)):
         first, count = rows[0] * mf, len(rows) * mf
         for side, dt, cross, crossed in ((0, 1, up_end, down_end), (1, -1, down_end, up_end)):
             here = pl.ds(first + (12 * mf if side == 0 else 0), count)
             going, coming = there(0, dt), there(0, -dt)
-            if rows[0] < 2:
+            if rows[0] == 0:
                 going, coming = going & ~cross, coming & ~crossed
             entry = send(
                 mbuf.at[:, here], edge.at[side, :, pl.ds(first, count)], 0, dt, going, coming,
@@ -233,10 +233,11 @@
         table[o, 8:24] = total
         if o % 4 in (0, 3):
             table_col[o % 4 // 3, o // 4] = total
-        if o < 4:
-            table_row[0, o : o + 1] = total[0:1]
-        if o >= 12:
-            table_row[1, o - 12 : o - 11] = total[15:16]
+        for x in (0, 128):
+            if o < 4:
+                scale_out[0, 16 + o : 17 + o, x : x + 128] = total[0:1]
+            if o >= 12:
+                scale_out[1, 4 + o : 5 + o, x : x + 128] = total[15:16]
     fetch_scale.wait()
     pack(scale, scale_out)
     source = lax.broadcasted_iota(jnp.int32, (384, 512), 0)
@@ -332,11 +333,6 @@
         if dt == 0:
             side = 1 if dm > 0 else 0
             rim_table.append(send_near(table_col.at[side], table_col_in.at[1 - side], dm, dt))
-        else:
-            side = 1 if dt > 0 else 0
-            rim_table.append(
-                send_near(table_row.at[side], table_row_in.at[1 - side, 1 - dm], dm, dt)
-            )
 
     rows = jnp.concatenate([coarse[q].reshape(64, 128) for q in range(4)], axis=1)
     out = split_dot(rows, perm[...])
@@ -483,7 +479,7 @@
 
     spans = [(0, 32), (64, 96), (32, 64)]
     shares = []
-    for low, high in spans:
+    for low, high in spans[:2]:
         shares.append(
             [
                 send(
@@ -493,10 +489,12 @@
                 for o in (1, 2, 3)
             ]
         )
-    shares[2] += [
-        send(part_x.at[lax.rem(m + o, groups)], got_x.at[o - 1], o, 0, start=False)
-        for o in (1, 2, 3)
-    ]
+    shares.append(
+        [
+            send(part_x.at[lax.rem(m + o, groups)], got_x.at[o - 1], o, 0, start=False)
+            for o in (1, 2, 3)
+        ]
+    )
     sub = lax.broadcasted_iota(jnp.int32, (4, 8, 128), 1)
     near32 = lax.broadcasted_iota(jnp.int32, (32, 128), 1) < 64
 
@@ -510,9 +508,13 @@
         out = split_dot(jnp.concatenate(folded, axis=1), perm[...], transposed=True)
         quarters = [out[:, 128 * q : 128 * q + 128] for q in range(4)]
         for q in range(4):
-            part[q, low:high] = quarters[q]
-            if piece == 2:
-                part_x[q] = jnp.where(near32, quarters[min(q + 1, 3)], quarters[max(q - 1, 0)])
+            if piece < 2:
+                part[q, low:high] = quarters[q]
+            else:
+                part_x[q, 0:32] = quarters[q]
+                part_x[q, 32:64] = jnp.where(
+                    near32, quarters[min(q + 1, 3)], quarters[max(q - 1, 0)]
+                )
         for copy, _, _ in shares[piece]:
             copy.start()
 
@@ -528,6 +530,7 @@
     share(2)
 
     wait_all(rim_table)
+    wait_all(rim_scale)
     near = lax.broadcasted_iota(jnp.int32, (16, 128), 1) < 64
     side_on = jnp.where(near, (m < groups - 1).astype(jnp.int32), (m > 0).astype(jnp.int32)) > 0
     for a in range(4):
@@ -538,8 +541,8 @@
         on = (t > 0) if side == 0 else (t < tiles - 1)
         row = 7 if side == 0 else 24
         for b in range(4):
-            table[first + b, row : row + 1] = jnp.where(on, table_row_in[side, 1, b : b + 1], 0.0)
-        both = jnp.where(near1, table_row_in[side, 2, 0:1], table_row_in[side, 0, 3:4])
+            table[first + b, row : row + 1] = jnp.where(on, scale_in[side, 16 + b : 17 + b, 128:256], 0.0)
+        both = jnp.where(near1, scale_in[side, 16:17, 384:512], scale_in[side, 19:20, 0:128])
         table_h[first // 4, row : row + 1] = jnp.where(side_on[0:1] & on, both, 0.0)
 
     rims = []
@@ -559,7 +562,6 @@
             rims.append(send_near(esum.at[1, 0:24], edown.at[slot], dm, dt))
 
     fetch_rate.wait()
-    wait_all(rim_scale)
     unpack(scale_in, scale)
     for f in range(FIELDS):
         p = jnp.where(inside, rimmed(scale, f) * rimmed(grad, f), 0.0)
@@ -571,7 +573,8 @@
         static_ref[f] = scale[f, 8:40, 128:384] * p[8:40, 0:256]
 
     wait_all(shares[2])
-    esum[1, 32:64] = (part[m, 32:64] + got[0, 32:64]) + (got[1, 32:64] + got[2, 32:64])
+    far = (part_x[m] + got_x[0]) + (got_x[1] + got_x[2])
+    esum[1, 32:64] = far[0:32]
     wait_all(rims)
     members_all = member_count * groups
 
@@ -587,7 +590,7 @@
     side_e = jnp.where(lane96 < 64, eall[2], eall[0]) / (members_all - 1)
     eall[1] = eall[1] / (members_all - 1)
     eall[0] = side_e
-    eall[0, 32:64] = ((part_x[m] + got_x[0]) + (got_x[1] + got_x[2])) / (members_all - 1)
+    eall[0, 32:64] = far[32:64] / (members_all - 1)
     for parity in range(2):
         pairs = [(1, 0), (3, -1)] if parity == 0 else [(2, 0), (0, 1)]
         for f in range(FIELDS):
@@ -624,7 +627,7 @@
     mf = member_count * FIELDS
     anywhere = pl.BlockSpec(memory_space=pl.ANY)
     vmem = pltpu.VMEM
-    sems = 80
+    sems = 54
     static, fine = pl.pallas_call(
         kernel,
         out_shape=[jax.ShapeDtypeStruct(gradient.shape, F32)] * 2,
@@ -635,14 +638,12 @@
             vmem((4, 48, 512), F32),
             vmem((2, 16, 256), F32),
             vmem((2, 16, 512), F32),
-            vmem((2, 16, 256), F32),
-            vmem((2, 16, 512), F32),
+            vmem((2, 24, 256), F32),
+            vmem((2, 24, 512), F32),
             vmem((4, 16, 128), jnp.int32),
             vmem((4, 16, 128), F32),
             vmem((2, 4, 16, 128), F32),
             vmem((2, 4, 16, 128), F32),
-            vmem((2, 8, 128), F32),
-            vmem((2, 3, 8, 128), F32),
             vmem((32, 512), F32),
             vmem(members.shape, BF16),
             vmem((512, 512), BF16),
@@ -667,9 +668,9 @@
             vmem((4, 24, 8, 128), F32),
             vmem((mf // 8, 4, 8, 8, 128), F32),
             vmem((4, 96, 128), F32),
-            vmem((4, 32, 128), F32),
+            vmem((4, 64, 128), F32),
             vmem((3, 96, 128), F32),
-            vmem((3, 32, 128), F32),
+            vmem((3, 64, 128), F32),
             vmem((3, 96, 128), F32),
             vmem((3, 24, 128), F32),
             vmem((3, 24, 128), F32),

time: 38.3 us -> 38 us (level)
  no operation moved by 1% of the time
where the time goes in v6:
time: 38 us; the launch traced here: 37.9 us
  Pallas kernels  37.2 us (98%)
  other arithmetic  0.68 us (2%)
    pallas_call x1, Pallas kernels, local(): pl.pallas_call(kernel, out_shape=[jax.ShapeDtypeStruct(gradient.shape, F3...  37.2 us

profile of v6, /device:TPU:33, one launch (start us, length us, event | category | flops | bytes accessed | tf_op | source)
XLA Modules:
  0.0 37.9 jit_solution(789214133913246827)
XLA Ops:
  0.0 37.2 %shard_map.73 = (f32[4,32,256]{2,1,0:T(8,128)S(1)}, f32[4,32,256]{2,1,0:T(8,128)S(1)}) custom-call(f32[4]{0:T(128)} %rate_hbm.1, f32[4,32,256]{2,1,0:T(8,128)} %grad_hbm.1, f32[4,32,256]{2,1,0:T(8,128)} %scale_hbm.1, s32[4,16,128]{2,1,0:T(8,128)} %index_hbm.1, f32[4,16,128]{2,1,0:T(8,128)} %weight_hbm.1, bf16[20,4,16,512]{3,2,1,0:T(8,128)(2,1)} %members_hbm.1, ...), custom_call_target="tpu_custom_call" | custom-call | tf_op jit(solution)/shard_map/pallas_call | solution.py:631
  37.2 0.7 %multiply_add_fusion = f32[4,32,256]{2,1,0:T(8,128)} fusion(f32[4,32,256]{2,1,0:T(8,128)S(1)} %get-tuple-element.8, f32[4,32,256]{2,1,0:T(8,128)S(1)} %get-tuple-element.7), kind=kLoop, calls=%fused_computation | loop fusion | flops 98304 | bytes 393216 | tf_op jit(solution)/shard_map/add | solution.py:689

commit v7 on v6

--- a/solution.py
+++ b/solution.py
@@ -16,6 +16,7 @@
 BF16 = jnp.bfloat16
 AROUND = [(0, 1), (0, -1), (1, 0), (-1, 0), (1, 1), (1, -1), (-1, 1), (-1, -1)]
 ZROW = 16
+SENDS = 41
 
 
 def split_dot(x, one_hot, transposed=False):
@@ -115,18 +116,27 @@
     fetch_scale = fetch(scale_hbm, scale.at[:, 8:40, 128:384])
 
     sent = []
+    slots, arrivals, slot_of = list(range(SENDS)), [], {}
 
     def send(src, dst, dm, dt, going=None, coming=None, start=True):
-        number = len(sent)
+        number = slots.pop(0)
+        arrivals.append(number)
         copy = pltpu.make_async_remote_copy(
-            src_ref=src, dst_ref=dst, send_sem=send_sem.at[number], recv_sem=recv_sem.at[number],
+            src_ref=src, dst_ref=dst, send_sem=send_sem.at[number], recv_sem=recv_sem.at[len(arrivals) - 1],
             device_id=at(dm, dt), device_id_type=MESH,
         )
         entry = (copy, going, coming)
+        slot_of[id(copy)] = number
         sent.append(entry)
         if start:
             only(entry[1], copy.start)
         return entry
+
+    def release(entries):
+        for entry in entries:
+            only(entry[1], entry[0].wait_send)
+            slots.insert(0, slot_of[id(entry[0])])
+        sent[:] = [kept for kept in sent if all(kept is not entry for entry in entries)]
 
     def send_near(src, dst, dm, dt):
         return send(src, dst, dm, dt, there(dm, dt), there(-dm, -dt))
@@ -323,6 +333,7 @@
         for f in range(FIELDS):
             coarse_out[0, q, 4 * f : 4 * f + 4] = coarse[q, f, 0:4]
             coarse_out[1, q, 4 * f : 4 * f + 4] = coarse[q, f, 12:16]
+    release(rim_grad + rim_spread + all_coarse)
     edge_coarse = [
         send_near(coarse_out.at[1], coarse_e.at[0], 0, 1),
         send_near(coarse_out.at[0], coarse_e.at[1], 0, -1),
@@ -627,7 +638,6 @@
     mf = member_count * FIELDS
     anywhere = pl.BlockSpec(memory_space=pl.ANY)
     vmem = pltpu.VMEM
-    sems = 54
     static, fine = pl.pallas_call(
         kernel,
         out_shape=[jax.ShapeDtypeStruct(gradient.shape, F32)] * 2,
@@ -679,8 +689,8 @@
             vmem((2, 128, 128), F32),
             pltpu.SMEM((4,), F32),
             pltpu.SemaphoreType.DMA((7,)),
-            pltpu.SemaphoreType.DMA((sems,)),
-            pltpu.SemaphoreType.DMA((sems,)),
+            pltpu.SemaphoreType.DMA((SENDS,)),
+            pltpu.SemaphoreType.DMA((54,)),
         ],
         compiler_params=pltpu.CompilerParams(
             collective_id=0, has_side_effects=True, vmem_limit_bytes=18 << 20

time: 38 us -> 37.9 us (level)
  no operation moved by 1% of the time
where the time goes in v7:
time: 37.9 us; the launch traced here: 37.8 us
  Pallas kernels  37.1 us (98%)
  other arithmetic  0.68 us (2%)
    pallas_call x1, Pallas kernels, local(): pl.pallas_call(kernel, out_shape=[jax.ShapeDtypeStruct(gradient.shape, F3...  37.1 us

profile of v7, /device:TPU:33, one launch (start us, length us, event | category | flops | bytes accessed | tf_op | source)
XLA Modules:
  0.0 37.8 jit_solution(664127494177142683)
XLA Ops:
  0.0 37.1 %shard_map.73 = (f32[4,32,256]{2,1,0:T(8,128)S(1)}, f32[4,32,256]{2,1,0:T(8,128)S(1)}) custom-call(f32[4]{0:T(128)} %rate_hbm.1, f32[4,32,256]{2,1,0:T(8,128)} %grad_hbm.1, f32[4,32,256]{2,1,0:T(8,128)} %scale_hbm.1, s32[4,16,128]{2,1,0:T(8,128)} %index_hbm.1, f32[4,16,128]{2,1,0:T(8,128)} %weight_hbm.1, bf16[20,4,16,512]{3,2,1,0:T(8,128)(2,1)} %members_hbm.1, ...), custom_call_target="tpu_custom_call" | custom-call | tf_op jit(solution)/shard_map/pallas_call | solution.py:641
  37.1 0.7 %multiply_add_fusion = f32[4,32,256]{2,1,0:T(8,128)} fusion(f32[4,32,256]{2,1,0:T(8,128)S(1)} %get-tuple-element.8, f32[4,32,256]{2,1,0:T(8,128)S(1)} %get-tuple-element.7), kind=kLoop, calls=%fused_computation | loop fusion | flops 98304 | bytes 393216 | tf_op jit(solution)/shard_map/add | solution.py:699
